TPU v7x, 256 devices: a whole 4x4x8 slice. The times are simulated.
256 devices in a mesh: dp: 8 (over y, z_hi), fsdp: 32 (over z_lo, x, core).
Axes of the slice: x: 4, y: 4, z: 8 (z_hi: 2, z_lo: 4; z = z_hi * 4 + z_lo), core: 2. Of those that a mesh axis runs over, the one named last changes fastest.
Arguments:
- tokens: bfloat16 [1024, 3072], P('dp'), may hold values from -6 to 6
- cotangent: bfloat16 [1024, 3072], P('dp'), may hold values from -6 to 6
- routes: int32 [1024, 2], P('dp'), may hold values from 0 to 7, all different within a row; in each aligned block of 128 rows (0 to 127, 128 to 255, ...) at most 48 rows name the same one
- router_weight: float32 [1024, 2], P('dp'), may hold values from 0.25 to 1
- w_gate: bfloat16 [8, 3072, 8192], P('dp', None, 'fsdp'), may hold values from -0.109375 to 0.109375
- w_up: bfloat16 [8, 3072, 8192], P('dp', None, 'fsdp'), may hold values from -0.109375 to 0.109375
- w_down: bfloat16 [8, 8192, 3072], P('dp', 'fsdp'), may hold values from -0.0625 to 0.0625
Outputs:
- output: bfloat16 [1024, 3072], P('dp')
- input_grad: bfloat16 [1024, 3072], P('dp')
- grad_gate: bfloat16 [8, 3072, 8192], P('dp', None, 'fsdp')
- grad_up: bfloat16 [8, 3072, 8192], P('dp', None, 'fsdp')
- grad_down: bfloat16 [8, 8192, 3072], P('dp', 'fsdp')
Inputs may be any that keep to these rules, and one draw needn't show every extreme that they name: `routes`: the two experts of a token differ. In the 128 rows of one batch no expert is named by more than 48 rows, a bound that some block reaches in some batches.
All inputs are finite; a program needn't handle non-finite values.
Results may differ from a plain program's by a relative error of at most 0.025.
Values may be sent and summed in bfloat16 or wider, within the bound.
A program may use at most 128 MiB of HBM per device.

v0:
```python
import jax
import jax.numpy as jnp
from jax import lax
from jax.sharding import PartitionSpec as P


def sent_together(arrays, axis, split_dim, concat_dim, along):
    both = jnp.concatenate(arrays, axis=along)
    filled, at, outs = (
        lax.all_to_all(both, axis, split_axis=split_dim, concat_axis=concat_dim, tiled=True),
        0,
        [],
    )
    for a in arrays:
        outs.append(lax.slice_in_dim(filled, at, at + a.shape[along], axis=along))
        at += a.shape[along]
    return tuple(outs)


def sent_together_2(arrays, axis, dim, along):
    both = jnp.concatenate(arrays, axis=along)
    filled, at, outs = (lax.psum_scatter(both, axis, scatter_dimension=dim, tiled=True), 0, [])
    for a in arrays:
        outs.append(lax.slice_in_dim(filled, at, at + a.shape[along], axis=along))
        at += a.shape[along]
    return tuple(outs)


def rows_first(arrays, axis, dims):
    turned = [jnp.moveaxis(a, dim, 0) for a, dim in zip(arrays, dims)]
    widths = [t[0].size for t in turned]
    both = jnp.concatenate([t.reshape(-1, w) for t, w in zip(turned, widths)], axis=1)
    filled = lax.all_gather(both, axis, axis=0, tiled=True)
    blocks = jnp.split(filled, [sum(widths[:k]) for k in range(1, len(widths))], axis=1)
    return tuple(
        (
            jnp.moveaxis(b.reshape(-1, *t.shape[1:]), 0, dim)
            for b, t, dim in zip(blocks, turned, dims)
        )
    )


def slot_tables(routes, router_weight, experts, capacity):
    expert_ids = jnp.arange(experts, dtype=jnp.int32)
    hit_table = (routes[:, :, None] == expert_ids).astype(jnp.int32)
    per_token = jnp.sum(hit_table, axis=1)
    before = jnp.cumsum(per_token, axis=0) - per_token
    slot_of = jnp.sum(hit_table * before[:, None, :], axis=2)
    slot_ids = jnp.arange(capacity, dtype=jnp.int32)
    placed = hit_table[:, :, :, None] * (slot_of[:, :, None, None] == slot_ids).astype(jnp.int32)
    tok_rows = routes.shape[0]
    flat = placed.reshape(tok_rows, 2, experts * capacity).astype(jnp.float32)
    slot_weight = jnp.sum(flat * router_weight[:, :, None], axis=(0, 1))
    return (flat[:, 0], flat[:, 1], slot_weight)


def on_device(tokens, cotangent, routes, router_weight, w_gate, w_up, w_down):
    experts = lax.axis_size("dp")
    tok_rows, features = tokens.shape
    capacity = max(tok_rows * 3 // 8, tok_rows * 2 // experts, 2)
    local_rows = experts * capacity
    lead = (((0,), (0,)), ((), ()))
    trail = (((1,), (1,)), ((), ()))
    first_pick, second_pick, slot_weight = slot_tables(routes, router_weight, experts, capacity)
    picked = (first_pick + second_pick).astype(jnp.bfloat16)
    send_x = lax.dot_general(picked, tokens, lead, preferred_element_type=jnp.float32).astype(
        jnp.bfloat16
    )
    chosen_dy = lax.dot_general(picked, cotangent, lead, preferred_element_type=jnp.float32)
    send_dy = (chosen_dy * slot_weight[:, None]).astype(jnp.bfloat16)
    arrived_x, arrived_dy = sent_together(
        (send_x.reshape(experts, capacity, features), send_dy.reshape(experts, capacity, features)),
        "dp",
        0,
        0,
        1,
    )
    slot_x = arrived_x.reshape(local_rows, features)
    slot_dy = arrived_dy.reshape(local_rows, features)
    gate_w = w_gate[0]
    up_w = w_up[0]
    down_w = w_down[0]
    gate_pre = jnp.dot(slot_x, gate_w, preferred_element_type=jnp.float32)
    up_pre = jnp.dot(slot_x, up_w, preferred_element_type=jnp.float32)
    sigma = jax.nn.sigmoid(gate_pre)
    active = gate_pre * sigma
    hidden = (active * up_pre).astype(jnp.bfloat16)
    out_terms = jnp.dot(hidden, down_w, preferred_element_type=jnp.float32)
    hidden_dy = lax.dot_general(slot_dy, down_w, trail, preferred_element_type=jnp.float32)
    gate_dy = (hidden_dy * up_pre * sigma * (1.0 + gate_pre * (1.0 - sigma))).astype(jnp.bfloat16)
    up_dy = (hidden_dy * active).astype(jnp.bfloat16)
    grad_down = lax.dot_general(hidden, slot_dy, lead, preferred_element_type=jnp.float32).astype(
        jnp.bfloat16
    )
    grad_gate = lax.dot_general(slot_x, gate_dy, lead, preferred_element_type=jnp.float32).astype(
        jnp.bfloat16
    )
    grad_up = lax.dot_general(slot_x, up_dy, lead, preferred_element_type=jnp.float32).astype(
        jnp.bfloat16
    )
    back_terms = lax.dot_general(
        gate_dy, gate_w, trail, preferred_element_type=jnp.float32
    ) + lax.dot_general(up_dy, up_w, trail, preferred_element_type=jnp.float32)
    out_part, back_part = tuple(
        (
            part.astype(jnp.float32)
            for part in sent_together_2(
                (
                    out_terms.reshape(experts, capacity, features).astype(jnp.bfloat16),
                    back_terms.reshape(experts, capacity, features).astype(jnp.bfloat16),
                ),
                "fsdp",
                2,
                0,
            )
        )
    )
    returned_out, returned_dx = sent_together(
        (out_part.astype(jnp.bfloat16), back_part.astype(jnp.bfloat16)), "dp", 0, 0, 1
    )
    width = out_part.shape[2]
    flat_out = returned_out.reshape(local_rows, width)
    flat_dx = returned_dx.reshape(local_rows, width)
    first_rows = jnp.dot(
        first_pick.astype(jnp.bfloat16), flat_out, preferred_element_type=jnp.float32
    )
    second_rows = jnp.dot(
        second_pick.astype(jnp.bfloat16), flat_out, preferred_element_type=jnp.float32
    )
    output = (router_weight[:, 0:1] * first_rows + router_weight[:, 1:2] * second_rows).astype(
        jnp.bfloat16
    )
    input_grad = jnp.dot(picked, flat_dx, preferred_element_type=jnp.float32).astype(jnp.bfloat16)
    output, input_grad = rows_first((output, input_grad), "fsdp", (1, 1))
    return (output, input_grad, grad_gate[None], grad_up[None], grad_down[None])


def solution(mesh):
    return jax.shard_map(
        on_device,
        mesh=mesh,
        in_specs=(
            P("dp", None),
            P("dp", None),
            P("dp", None),
            P("dp", None),
            P("dp", None, "fsdp"),
            P("dp", None, "fsdp"),
            P("dp", "fsdp", None),
        ),
        out_specs=(
            P("dp", None),
            P("dp", None),
            P("dp", None, "fsdp"),
            P("dp", None, "fsdp"),
            P("dp", "fsdp", None),
        ),
        check_vma=False,
    )
```

profile of v0, /device:TPU:1, one launch (start us, length us, event | category | flops | bytes accessed | tf_op | source)
XLA Modules:
  0.0 411.4 jit_solution(14644520533077346576)
XLA Ops:
  7.2 0.0 copy-start
  7.2 0.0 reduce-scatter.4.cloned.1.call-start
  7.2 0.8 fusion.23
  8.0 0.7 fusion.22
  8.7 0.1 copy.22
  8.8 0.2 reduce_window_sum.11
  9.0 0.7 select_reduce_fusion
  9.8 0.8 multiply_reduce_fusion
  10.6 0.1 mul.95
  10.7 1.9 convolution_convert_fusion
  12.6 0.0 copy-done.7
  12.6 0.8 multiply_convert_fusion
  13.4 0.3 pad_maximum_fusion
  13.8 88.1 %all_to_all.10 = bf16[8,96,3072]{2,1,0:T(8,128)(2,1)S(1)} all-to-all(bf16[8,96,3072]{2,1,0:T(8,128)(2,1)S(1)} %pad_maximum_fusion), channel_id=1, replica_groups=mesh['dp'=8,'fsdp'=32] {'dp'}, dimensions={0} | all-to-all | bytes 9437184 | tf_op jit(solution)/shard_map/all_to_all | solution.py:10
  101.8 0.4 fusion.24
  102.3 1.0 copy-done.5
  103.2 0.8 fusion.4
  104.1 1.2 copy-done.6
  105.3 0.8 fusion.11
  106.1 0.9 multiply_convert_fusion.3
  107.0 0.8 convolution_convert_fusion.1
  107.8 0.8 fusion.9
  108.6 0.8 add_convert_fusion
  109.4 2.5 pad_maximum_fusion.1
  111.9 14.9 %copy.30 = bf16[16,48,3072]{1,0,2:T(8,128)(2,1)} copy(bf16[16,48,3072]{2,1,0:T(8,128)(2,1)} %pad_maximum_fusion.1) | data formatting | bytes 9437184
  126.9 18.1 %reshape.77 = bf16[3072,768]{1,0:T(8,128)(2,1)} reshape(bf16[3072,16,48]{2,1,0:T(8,128)(2,1)} %bitcast.76) | data formatting | bytes 9437184
  145.0 0.0 reduce-scatter.4.cloned.1.call-update
  145.0 0.0 copy-start.8
  145.0 177.5 %reduce-scatter.4.cloned.1.call-done = bf16[96,768]{1,0:T(8,128)(2,1)} async-done(((bf16[3072,768]{1,0:T(8,128)(2,1)}), bf16[96,768]{1,0:T(8,128)(2,1)}) %reduce-scatter.4.cloned.1.call-update) | async-done | bytes 147472
  322.6 1.4 reshape.78
  324.0 0.2 copy.32
  324.1 0.2 copy.33
  324.3 0.7 pad_maximum_fusion.2
  325.0 7.8 %all-to-all-start.1 = ((bf16[8,96,96]{2,1,0:T(8,128)(2,1)}), bf16[8,96,96]{2,1,0:T(8,128)(2,1)S(1)}, u32[]{:S(2)}, u32[]{:S(2)}) async-start(bf16[8,96,96]{2,1,0:T(8,128)(2,1)} %pad_maximum_fusion.2), calls=%async_computation.1 | async-start | bytes 393216 | tf_op jit(solution)/shard_map/all_to_all | solution.py:10
  332.8 0.2 all-gather.2.cloned.1.call-start
  333.0 9.5 %all-to-all-done.1 = bf16[8,96,96]{2,1,0:T(8,128)(2,1)S(1)} async-done(((bf16[8,96,96]{2,1,0:T(8,128)(2,1)}), bf16[8,96,96]{2,1,0:T(8,128)(2,1)S(1)}, u32[]{:S(2)}, u32[]{:S(2)}) %all-to-all-start.1) | async-done | bytes 147488 | tf_op jit(solution)/shard_map/all_to_all | solution.py:10
  342.5 0.2 convolution_convert_fusion.5
  342.7 0.2 convolution_multiply_fusion.1
  342.9 0.2 fusion.14
  343.1 0.6 pad_maximum_fusion.3
  343.8 0.0 all-gather.2.cloned.1.call-update
  343.8 3.8 fusion.2
  347.6 4.0 fusion
  351.6 2.2 fusion.1
  353.8 46.9 %all-gather.2.cloned.1.call-done = bf16[3072,256]{1,0:T(8,128)(2,1)} async-done(((bf16[96,256]{1,0:T(8,128)(2,1)}), bf16[3072,256]{1,0:T(8,128)(2,1)}) %all-gather.2.cloned.1.call-update) | async-done | bytes 1572880 | tf_op jit(solution)/shard_map/all_gather | solution.py:33
  400.7 1.6 slice_bitcast_fusion
  402.3 1.2 copy.29
  403.4 1.2 copy.28
  (21 shorter events, 0.2 us)
Async XLA Ops:
  7.2 99.0 %copy-start = (bf16[1,3072,256]{2,1,0:T(8,128)(2,1)S(1)}, bf16[1,3072,256]{2,1,0:T(8,128)(2,1)}, u32[]{:S(2)}) copy-start(bf16[1,3072,256]{2,1,0:T(8,128)(2,1)} %param.12) | copy-start | bytes 4718596
  7.2 315.4 %reduce-scatter.4.cloned.1.call-start = ((), (), s32[]{:S(2)}) async-start(), calls=%async_computation.4 | async-start | bytes 4866048
  8.8 3.8 copy-start.7
  101.8 1.4 copy-start.5
  102.3 1.8 copy-start.2
  102.3 3.8 copy-start.3
  103.2 2.1 copy-start.6
  145.0 188.0 %copy-start.8 = (f32[128,2]{0,1:T(2,128)S(1)}, f32[128,2]{0,1:T(2,128)}, u32[]{:S(2)}) copy-start(f32[128,2]{0,1:T(2,128)} %param.10) | copy-start | bytes 3076
  325.0 17.5 %all-to-all-start.1 = ((bf16[8,96,96]{2,1,0:T(8,128)(2,1)}), bf16[8,96,96]{2,1,0:T(8,128)(2,1)S(1)}, u32[]{:S(2)}, u32[]{:S(2)}) async-start(bf16[8,96,96]{2,1,0:T(8,128)(2,1)} %pad_maximum_fusion.2), calls=%async_computation.1 | async-start | bytes 393216 | tf_op jit(solution)/shard_map/all_to_all | solution.py:10
  332.8 67.9 %all-gather.2.cloned.1.call-start = ((), (), s32[]{:S(2)}) async-start(), calls=%async_computation.3 | async-start | bytes 1622016 | tf_op jit(solution)/shard_map/all_gather | solution.py:33
  347.6 4.0 copy-start.4
  400.7 3.9 copy-start.1
Sparse Core Ops, SparseCore 0:
  145.1 177.3 reduce-scatter.3
  343.9 56.7 all-gather.1
where the time goes:
time: 413 us; the launch traced here: 411 us
  waiting for transfers between devices  234 us (57%)
  blocking collectives  88.1 us (21%)
  local copies, waits for them, and re-layouts  41.6 us (10%)
  matrix products  18.1 us (4%)
  between operations  14.3 us (3%)
  starting transfers between devices  8.02 us (2%)
  other arithmetic  7.43 us (2%)
    unnamed x3, waiting for transfers between devices  178 us
    all_to_all x1, blocking collectives, sent_together(): lax.all_to_all(both, axis, split_axis=split_dim, concat_axis=concat_dim,...  88.1 us
    all_gather x1, waiting for transfers between devices, rows_first(): filled = lax.all_gather(both, axis, axis=0, tiled=True)  46.9 us
    unnamed x25, local copies, waits for them, and re-layouts  39.3 us
    all_to_all x1, waiting for transfers between devices, sent_together(): lax.all_to_all(both, axis, split_axis=split_dim, concat_axis=concat_dim,...  9.47 us
  transfers between devices with their start and end apart: 3, of which 3 were waited for; matrix products, arithmetic and copies ran while one was open for 2% of the time, Pallas kernels for 0%

commit v1 on v0

v1 whole, which is shorter than its diff:
```python
import functools

import jax
import jax.numpy as jnp
from jax import lax
from jax.experimental import pallas as pl
from jax.experimental.pallas import tpu as pltpu
from jax.sharding import PartitionSpec as P

MESH = pl.DeviceIdType.MESH
NY, NZH, NZ, NX, NC = 4, 2, 4, 4, 2
BF, F32 = jnp.bfloat16, jnp.float32
TRAIL = (((1,), (1,)), ((), ()))
LEAD = (((0,), (0,)), ((), ()))


class Dims:
    def __init__(self, tok, feat, hid):
        self.tok, self.feat, self.hid = tok, feat, hid
        self.cap = tok * 3 // 8
        self.grp = NY * self.cap
        self.quart = feat // NX
        self.half = self.quart // 2
        self.tile = self.quart // 6


def experts_kernel(
    dims,
    send, first_pick, second_pick, pick_w, gate_hbm, up_hbm, down_hbm,
    out_hbm, gg_hbm, gu_hbm, gd_hbm,
    arr, wg, wu, wd, hid, gdy, udy, tt, dd, rl1, rr1, rl2, rr2, yy, zr, ww, uu, outs, gg, gu, gd,
    ss, rs, ls,
):
    cap, grp, quart, half, tile = dims.cap, dims.grp, dims.quart, dims.half, dims.tile
    dp, fs = lax.axis_index("dp"), lax.axis_index("fsdp")
    y, zh = dp // 2, dp % 2
    z, x, k = fs // 8, (fs // 2) % 4, fs % 2
    other = 1 - k

    def dev(yy_, zh_, z_, x_, k_):
        return (yy_ * 2 + zh_, (z_ * 4 + x_) * 2 + k_)

    def up_y(d):
        return (y + d) % 4

    right, left = dev(y, zh, z, (x + 1) % 4, k), dev(y, zh, z, (x + 3) % 4, k)
    sibling = dev(y, zh, z, x, other)

    used = [0]
    pending = []

    def fresh():
        used[0] += 1
        return used[0] - 1

    def copy(i, src, dst, to):
        return pltpu.make_async_remote_copy(
            src_ref=src, dst_ref=dst, send_sem=ss.at[i], recv_sem=rs.at[i],
            device_id=to, device_id_type=MESH,
        )

    def push(i, src, dst, to):
        c = copy(i, src, dst, to)
        c.start()
        pending.append(c)

    def got(i, region):
        copy(i, region, region, sibling).wait_recv()

    def qcols(q, off=0, width=None):
        return pl.ds(pl.multiple_of(q * quart + off, 128), quart if width is None else width)

    def rows_of(b):
        return pl.ds(pl.multiple_of(b * cap, 16), cap)

    loads = [
        pltpu.make_async_copy(s, d, ls.at[n])
        for n, (s, d) in enumerate(((gate_hbm, wg), (up_hbm, wu), (down_hbm, wd)))
    ]
    for c in loads:
        c.start()

    barrier = pltpu.get_barrier_semaphore()
    partners = [right, left, sibling]
    for d in range(1, 4):
        partners.append(dev(y, zh, (z + d) % 4, x, k))
    for d in range(4):
        if d:
            partners.append(dev(up_y(d), zh, z, x, k))
        partners.append(dev(up_y(d), 1 - zh, z, x, k))
    for p in partners:
        pl.semaphore_signal(barrier, inc=1, device_id=p, device_id_type=MESH)
    pl.semaphore_wait(barrier, len(partners))

    zc = 1 - zh
    cross_ids, same_ids, both_ids = {}, {}, {}
    for d in (0, 1, 3, 2):
        cross_ids[d] = fresh()
        push(
            cross_ids[d],
            send.at[zc, rows_of(up_y(d)), qcols(x)],
            arr.at[k, zh, rows_of(y), qcols(x)],
            dev(up_y(d), zc, z, x, k),
        )
    for d in (1, 3, 2):
        same_ids[d] = fresh()
        push(
            same_ids[d],
            send.at[zh, rows_of(up_y(d))],
            arr.at[k, zh, rows_of(y)],
            dev(up_y(d), zh, z, x, k),
        )
    for g in range(2):
        for d in range(4):
            both_ids[g, d] = fresh()
    push(both_ids[0, 0], send.at[zh, rows_of(y)], arr.at[k, zh, rows_of(y)], sibling)
    arr[k, zh, rows_of(y)] = send[zh, rows_of(y)]
    for d in (1, 3, 2):
        block = arr.at[k, zh, rows_of(up_y(4 - d))]
        got(same_ids[d], block)
        push(both_ids[0, d], block, block, sibling)
    ring = {}
    for d in (0, 1, 3, 2):
        rows = rows_of(up_y(4 - d))
        mine = arr.at[k, zc, rows, qcols(x)]
        got(cross_ids[d], mine)
        ring[d] = [fresh() for _ in range(4)]
        push(ring[d][0], mine, mine, right)
        push(ring[d][1], mine, mine, left)

    def first_stage(g):
        zg = zh if g == 0 else zc
        gate_pre = jnp.dot(arr[0, zg], wg[...], preferred_element_type=F32)
        up_pre = jnp.dot(arr[0, zg], wu[...], preferred_element_type=F32)
        hidden_dy = lax.dot_general(arr[1, zg], wd[...], TRAIL, preferred_element_type=F32)
        sigma = jax.nn.sigmoid(gate_pre)
        active = gate_pre * sigma
        hid[zg] = (active * up_pre).astype(BF)
        gdy[zg] = (hidden_dy * up_pre * sigma * (1.0 + gate_pre * (1.0 - sigma))).astype(BF)
        udy[zg] = (hidden_dy * active).astype(BF)

    quarters = [(x + 2) % 4, (x + 1) % 4, (x + 3) % 4, x]
    swap_ids = {(g, n): fresh() for g in range(2) for n in range(4)}

    def second_stage(g):
        zg = zh if g == 0 else zc
        width = quart // 3
        for n, q in enumerate(quarters):

            def body(c, carry, q=q):
                at = pl.ds(pl.multiple_of(q * quart + c * width, 128), width)
                tt[g, 0, :, at] = jnp.dot(
                    hid[zg], wd[:, at], preferred_element_type=F32
                ).astype(BF)
                tt[g, 1, :, at] = (
                    lax.dot_general(gdy[zg], wg[at, :], TRAIL, preferred_element_type=F32)
                    + lax.dot_general(udy[zg], wu[at, :], TRAIL, preferred_element_type=F32)
                ).astype(BF)
                return carry

            lax.fori_loop(0, 3, body, 0)
            push(swap_ids[g, n], tt.at[g, other, :, qcols(q)], dd.at[g, :, qcols(q)], sibling)

    def plus(a, b):
        return (a.astype(F32) + b.astype(F32)).astype(BF)

    hop_ids = {(g, n): fresh() for g in range(2) for n in range(6)}

    def chip_sum(g, n):
        q = quarters[n]
        got(swap_ids[g, n], dd.at[g, :, qcols(q)])
        tt[g, k, :, qcols(q)] = plus(tt[g, k, :, qcols(q)], dd[g, :, qcols(q)])

    def hop_one(g):
        chip_sum(g, 0)
        far = quarters[0]
        push(hop_ids[g, 0], tt.at[g, k, :, qcols(far, 0, half)], rl1.at[g], right)
        push(hop_ids[g, 1], tt.at[g, k, :, qcols(far, half, half)], rr1.at[g], left)
        chip_sum(g, 1)
        push(
            hop_ids[g, 2], tt.at[g, k, :, qcols(quarters[1], half, half)],
            rl2.at[g, :, pl.ds(half, half)], right,
        )
        chip_sum(g, 2)
        push(
            hop_ids[g, 3], tt.at[g, k, :, qcols(quarters[2], 0, half)],
            rr2.at[g, :, pl.ds(0, half)], left,
        )
        chip_sum(g, 3)

    def hop_two(g):
        got(hop_ids[g, 0], rl1.at[g])
        at = qcols(quarters[1], 0, half)
        tt[g, k, :, at] = plus(tt[g, k, :, at], rl1[g])
        push(hop_ids[g, 4], tt.at[g, k, :, at], rl2.at[g, :, pl.ds(0, half)], right)
        got(hop_ids[g, 1], rr1.at[g])
        at = qcols(quarters[2], half, half)
        tt[g, k, :, at] = plus(tt[g, k, :, at], rr1[g])
        push(hop_ids[g, 5], tt.at[g, k, :, at], rr2.at[g, :, pl.ds(half, half)], left)

    def head(zz):
        return (3 * zz + 1 - k) // 2

    def pair(zz):
        return (zz + k) % 2 == 0

    def tcols(t, base=0):
        return pl.ds(pl.multiple_of(base + t * tile, 128), tile)

    tile_ids = {(g, d, s): fresh() for g in range(2) for d in range(1, 4) for s in range(2)}

    def along_z(g):
        for n in (2, 3, 4, 5):
            region = (rl2 if n in (2, 4) else rr2).at[
                g, :, pl.ds(half if n in (2, 5) else 0, half)
            ]
            got(hop_ids[g, n], region)
        yy[g] = (
            tt[g, k, :, qcols(x)].astype(F32) + rl2[g].astype(F32) + rr2[g].astype(F32)
        ).astype(BF)
        for d in range(1, 4):
            zz = (z + d) % 4
            to = dev(y, zh, zz, x, k)
            push(tile_ids[g, d, 0], yy.at[g, :, tcols(head(zz))], zr.at[g, d - 1, 0], to)

            @pl.when(pair(zz))
            def _(d=d, zz=zz, to=to):
                copy(
                    tile_ids[g, d, 1], yy.at[g, :, tcols(head(zz) + 1)], zr.at[g, d - 1, 1], to
                ).start()

    back_ids = {(g, d): fresh() for g in range(2) for d in range(4)}

    def home(g):
        zg = zh if g == 0 else zc

        def summed(s):
            total = yy[g, :, tcols(head(z) + s)].astype(F32)
            for d in range(1, 4):
                total = total + zr[g, d - 1, s].astype(F32)
            ww[g, :, pl.ds(s * tile, tile)] = total.astype(BF)

        for d in range(1, 4):
            got(tile_ids[g, d, 0], zr.at[g, d - 1, 0])
        summed(0)

        @pl.when(pair(z))
        def _():
            for d in range(1, 4):
                got(tile_ids[g, d, 1], zr.at[g, d - 1, 1])
            summed(1)

        @pl.when(jnp.logical_not(pair(z)))
        def _():
            ww[g, :, pl.ds(tile, tile)] = jnp.zeros((grp, tile), BF)

        for d in (1, 3, 2, 0):
            if g == 0 and d == 0:
                uu[zh, rows_of(y)] = ww[0, rows_of(y)]
            else:
                push(
                    back_ids[g, d], ww.at[g, rows_of(up_y(d))], uu.at[zh, rows_of(y)],
                    dev(up_y(d), zg, z, x, k),
                )

    grad_copies = []

    def weight_grads():
        width = 256
        rows = 2 * grp

        def body(c, carry):
            at = pl.ds(pl.multiple_of(c * width, 128), width)
            xs = arr[0, :, :, at].reshape(rows, width)
            ys = arr[1, :, :, at].reshape(rows, width)
            hidden = hid[...].reshape(rows, dims.hid)
            gg[at, :] = lax.dot_general(
                xs, gdy[...].reshape(rows, dims.hid), LEAD, preferred_element_type=F32
            ).astype(BF)
            gu[at, :] = lax.dot_general(
                xs, udy[...].reshape(rows, dims.hid), LEAD, preferred_element_type=F32
            ).astype(BF)
            gd[:, at] = lax.dot_general(
                hidden, ys, LEAD, preferred_element_type=F32
            ).astype(BF)
            return carry

        lax.fori_loop(0, dims.feat // width, body, 0)
        for n, (s, d) in enumerate(((gg, gg_hbm), (gu, gu_hbm), (gd, gd_hbm))):
            c = pltpu.make_async_copy(s, d, ls.at[3 + n])
            c.start()
            grad_copies.append(c)

    for c in loads:
        c.wait()
    for d in range(4):
        got(both_ids[0, d], arr.at[other, zh, rows_of(up_y(4 - d) if d else y)])
    first_stage(0)
    for d in (0, 1, 3, 2):
        rows = rows_of(up_y(4 - d))
        from_left = arr.at[k, zc, rows, qcols((x + 3) % 4)]
        from_right = arr.at[k, zc, rows, qcols((x + 1) % 4)]
        got(ring[d][0], from_left)
        got(ring[d][1], from_right)
        near = arr.at[k, zc, rows, qcols((x + 3) % 4, 0, half)]
        push(ring[d][2], near, near, right)
        near = arr.at[k, zc, rows, qcols((x + 1) % 4, half, half)]
        push(ring[d][3], near, near, left)
    second_stage(0)
    for d in (0, 1, 3, 2):
        rows = rows_of(up_y(4 - d))
        got(ring[d][2], arr.at[k, zc, rows, qcols((x + 2) % 4, 0, half)])
        got(ring[d][3], arr.at[k, zc, rows, qcols((x + 2) % 4, half, half)])
        block = arr.at[k, zc, rows]
        push(both_ids[1, d], block, block, sibling)
    hop_one(0)
    for d in range(4):
        got(both_ids[1, d], arr.at[other, zc, rows_of(up_y(4 - d) if d else y)])
    first_stage(1)
    second_stage(1)
    hop_two(0)
    hop_one(1)
    weight_grads()
    along_z(0)
    hop_two(1)
    home(0)
    along_z(1)
    home(1)

    for g in range(2):
        zg = zh if g == 0 else zc
        for d in range(4):
            if g or d:
                got(back_ids[g, d], uu.at[zg, rows_of(up_y(4 - d) if d else y)])
    slots = uu[...].reshape(2 * grp, 2 * tile)
    mixed = (
        pick_w[:, 0:1] * jnp.dot(first_pick[...], slots, preferred_element_type=F32)
        + pick_w[:, 1:2] * jnp.dot(second_pick[...], slots, preferred_element_type=F32)
    ).astype(BF)
    base = x * quart
    outs[k, :, tcols(head(z), base)] = mixed[:, :tile]

    @pl.when(pair(z))
    def _():
        outs[k, :, tcols(head(z) + 1, base)] = mixed[:, tile:]

    last_ids = {(d, s): fresh() for d in range(1, 4) for s in range(2)}
    for d in range(1, 4):
        mine = outs.at[k, :, tcols(head(z), base)]
        to = dev(y, zh, (z + d) % 4, x, k)
        push(last_ids[d, 0], mine, mine, to)

        @pl.when(pair(z))
        def _(d=d, to=to):
            second = outs.at[k, :, tcols(head(z) + 1, base)]
            copy(last_ids[d, 1], second, second, to).start()

    for d in range(1, 4):
        zz = (z + 4 - d) % 4
        got(last_ids[d, 0], outs.at[k, :, tcols(head(zz), base)])

        @pl.when(pair(zz))
        def _(d=d, zz=zz):
            got(last_ids[d, 1], outs.at[k, :, tcols(head(zz) + 1, base)])

    turn = [fresh() for _ in range(4)]
    share = [fresh() for _ in range(4)]
    mine = outs.at[k, :, qcols(x)]
    push(turn[0], mine, mine, right)
    push(turn[1], mine, mine, left)
    push(share[0], mine, mine, sibling)
    from_left = outs.at[k, :, qcols((x + 3) % 4)]
    from_right = outs.at[k, :, qcols((x + 1) % 4)]
    got(turn[0], from_left)
    near = outs.at[k, :, qcols((x + 3) % 4, 0, half)]
    push(turn[2], near, near, right)
    push(share[1], from_left, from_left, sibling)
    got(turn[1], from_right)
    near = outs.at[k, :, qcols((x + 1) % 4, half, half)]
    push(turn[3], near, near, left)
    push(share[2], from_right, from_right, sibling)
    opposite = outs.at[k, :, qcols((x + 2) % 4)]
    got(turn[2], outs.at[k, :, qcols((x + 2) % 4, 0, half)])
    got(turn[3], outs.at[k, :, qcols((x + 2) % 4, half, half)])
    push(share[3], opposite, opposite, sibling)
    for n, q in enumerate((x, (x + 3) % 4, (x + 1) % 4, (x + 2) % 4)):
        got(share[n], outs.at[other, :, qcols(q)])
    final = pltpu.make_async_copy(outs, out_hbm, ls.at[6])
    final.start()
    for c in pending:
        c.wait_send()
    for g in range(2):
        for d in range(1, 4):
            zz = (z + d) % 4

            @pl.when(pair(zz))
            def _(g=g, d=d, zz=zz):
                copy(
                    tile_ids[g, d, 1], yy.at[g, :, tcols(head(zz) + 1)], zr.at[g, d - 1, 1],
                    sibling,
                ).wait_send()

    @pl.when(pair(z))
    def _():
        for d in range(1, 4):
            second = outs.at[k, :, tcols(head(z) + 1, base)]
            copy(last_ids[d, 1], second, second, sibling).wait_send()

    for c in grad_copies:
        c.wait()
    final.wait()


def slot_tables(routes, router_weight, order, capacity):
    hit_table = (routes[:, :, None] == order).astype(jnp.int32)
    per_token = jnp.sum(hit_table, axis=1)
    before = jnp.cumsum(per_token, axis=0) - per_token
    slot_of = jnp.sum(hit_table * before[:, None, :], axis=2)
    slot_ids = jnp.arange(capacity, dtype=jnp.int32)
    placed = hit_table[:, :, :, None] * (slot_of[:, :, None, None] == slot_ids).astype(jnp.int32)
    tok_rows = routes.shape[0]
    flat = placed.reshape(tok_rows, 2, order.shape[0] * capacity).astype(jnp.float32)
    slot_weight = jnp.sum(flat * router_weight[:, :, None], axis=(0, 1))
    return (flat[:, 0], flat[:, 1], slot_weight)


def on_device(tokens, cotangent, routes, router_weight, w_gate, w_up, w_down):
    experts = lax.axis_size("dp")
    dims = Dims(tokens.shape[0], tokens.shape[1], w_gate.shape[2])
    cap, grp = dims.cap, dims.grp
    core = lax.axis_index("fsdp") % 2
    order = jnp.arange(experts, dtype=jnp.int32).reshape(NY, NZH).T.reshape(-1)
    first_pick, second_pick, slot_weight = slot_tables(routes, router_weight, order, cap)
    picked = (first_pick + second_pick).astype(BF)
    mine = jnp.where(core == 0, tokens, cotangent)
    scale = jnp.where(core == 0, 1.0, slot_weight)
    rows = lax.dot_general(picked, mine, LEAD, preferred_element_type=F32)
    send = (rows * scale[:, None]).astype(BF).reshape(2, grp, dims.feat)
    pick_w = jnp.where(core == 0, router_weight, 1.0)
    vmem = pl.BlockSpec(memory_space=pltpu.VMEM)
    hbm = pl.BlockSpec(memory_space=pl.ANY)
    feat, hid, half, quart, tile = dims.feat, dims.hid, dims.half, dims.quart, dims.tile
    outs, gg, gu, gd = pl.pallas_call(
        functools.partial(experts_kernel, dims),
        out_shape=(
            jax.ShapeDtypeStruct((2, dims.tok, feat), BF),
            jax.ShapeDtypeStruct((feat, hid), BF),
            jax.ShapeDtypeStruct((feat, hid), BF),
            jax.ShapeDtypeStruct((hid, feat), BF),
        ),
        in_specs=[vmem] * 4 + [hbm] * 3,
        out_specs=(hbm,) * 4,
        scratch_shapes=[
            pltpu.VMEM((2, 2, grp, feat), BF),
            pltpu.VMEM((feat, hid), BF),
            pltpu.VMEM((feat, hid), BF),
            pltpu.VMEM((hid, feat), BF),
            pltpu.VMEM((2, grp, hid), BF),
            pltpu.VMEM((2, grp, hid), BF),
            pltpu.VMEM((2, grp, hid), BF),
            pltpu.VMEM((2, 2, grp, feat), BF),
            pltpu.VMEM((2, grp, feat), BF),
            pltpu.VMEM((2, grp, half), BF),
            pltpu.VMEM((2, grp, half), BF),
            pltpu.VMEM((2, grp, quart), BF),
            pltpu.VMEM((2, grp, quart), BF),
            pltpu.VMEM((2, grp, quart), BF),
            pltpu.VMEM((2, 3, 2, grp, tile), BF),
            pltpu.VMEM((2, grp, 2 * tile), BF),
            pltpu.VMEM((2, grp, 2 * tile), BF),
            pltpu.VMEM((2, dims.tok, feat), BF),
            pltpu.VMEM((feat, hid), BF),
            pltpu.VMEM((feat, hid), BF),
            pltpu.VMEM((hid, feat), BF),
            pltpu.SemaphoreType.DMA((96,)),
            pltpu.SemaphoreType.DMA((96,)),
            pltpu.SemaphoreType.DMA((7,)),
        ],
        compiler_params=pltpu.CompilerParams(
            collective_id=0, has_side_effects=True, vmem_limit_bytes=60 * 1024 * 1024
        ),
        name="experts",
    )(send, first_pick.astype(BF), second_pick.astype(BF), pick_w, w_gate[0], w_up[0], w_down[0])
    return (outs[0], outs[1], gg[None], gu[None], gd[None])


def solution(mesh):
    return jax.shard_map(
        on_device,
        mesh=mesh,
        in_specs=(
            P("dp", None),
            P("dp", None),
            P("dp", None),
            P("dp", None),
            P("dp", None, "fsdp"),
            P("dp", None, "fsdp"),
            P("dp", "fsdp", None),
        ),
        out_specs=(
            P("dp", None),
            P("dp", None),
            P("dp", None, "fsdp"),
            P("dp", None, "fsdp"),
            P("dp", "fsdp", None),
        ),
        check_vma=False,
    )
```

time: 413 us -> 117 us (0.28)
  waiting for transfers between devices: 234 us -> 0 us
  Pallas kernels: 0 us -> 98.7 us
  blocking collectives: 88.1 us -> 0 us
  local copies, waits for them, and re-layouts: 41.6 us -> 9.22 us
  matrix products: 18.1 us -> 2.22 us
  between operations: 14.3 us -> 0.72 us
  starting transfers between devices: 8.02 us -> 0 us
    unnamed x3 -> x0, waiting for transfers between devices: 178 us -> none
    pallas_call x0 -> x1, Pallas kernels: none -> 98.7 us  [on_device(): pl.pallas_call(functools.partial(experts_kernel, dims), out_shape=(jax.Sh...]
    all_to_all x1 -> x0, blocking collectives: 88.1 us -> none  [sent_together(): lax.all_to_all(both, axis, split_axis=split_dim, concat_axis=concat_dim,...]
    all_gather x1 -> x0, waiting for transfers between devices: 46.9 us -> none  [rows_first(): filled = lax.all_gather(both, axis, axis=0, tiled=True)]
    unnamed x25 -> x16, local copies, waits for them, and re-layouts: 39.3 us -> 6.15 us
    dot_general x14 -> x1, matrix products: 18.1 us -> 2.22 us  [on_device(): rows = lax.dot_general(picked, mine, LEAD, preferred_element_type=F32)]
    all_to_all x1 -> x0, waiting for transfers between devices: 9.47 us -> none  [sent_together(): lax.all_to_all(both, axis, split_axis=split_dim, concat_axis=concat_dim,...]
    all_to_all x1 -> x0, starting transfers between devices: 7.77 us -> none  [sent_together(): lax.all_to_all(both, axis, split_axis=split_dim, concat_axis=concat_dim,...]
  transfers between devices with their start and end apart: 3 -> 0, of which waited for: 3 -> 0; matrix products, arithmetic and copies ran while one was open for 2% -> 0% of each run, Pallas kernels for 0% -> 0%
where the time goes in v1:
time: 117 us; the launch traced here: 116 us
  Pallas kernels  98.7 us (84%)
  local copies, waits for them, and re-layouts  9.22 us (8%)
  other arithmetic  4.76 us (4%)
  matrix products  2.22 us (2%)
    pallas_call x1, Pallas kernels, on_device(): pl.pallas_call(functools.partial(experts_kernel, dims), out_shape=(jax.Sh...  98.7 us
    unnamed x16, local copies, waits for them, and re-layouts  6.15 us
    squeeze x1, local copies, waits for them, and re-layouts, on_device(): return (outs[0], outs[1], gg[None], gu[None], gd[None])  2.73 us

profile of v1, /device:TPU:1, one launch (start us, length us, event | category | flops | bytes accessed | tf_op | source)
XLA Modules:
  0.0 115.6 jit_solution(18208398093798574845)
XLA Ops:
  0.7 0.1 reshape.84
  0.7 0.8 fusion.6
  1.5 0.7 compare_convert_fusion
  2.2 0.1 copy.17
  2.3 0.2 reduce_window_sum.11
  2.5 0.0 copy-start.3
  2.5 0.0 copy-start.4
  2.6 0.9 fusion.5
  3.5 0.8 multiply_reduce_fusion
  4.3 0.1 select_n.43
  4.4 0.8 copy.22
  5.2 0.6 broadcast_select_fusion.pick_w
  5.9 0.1 copy.24
  6.0 0.1 copy.23
  6.1 0.7 convert_bitcast_fusion
  6.9 0.0 copy-done.3
  6.9 0.0 copy-done.4
  6.9 2.2 %multiply_convert_fusion = bf16[384,3072]{1,0:T(8,128)(2,1)} fusion(f32[384]{0:T(512)S(1)} %select_n.43, bf16[128,3072]{1,0:T(8,128)(2,1)S(1)} %copy-done.3, bf16[128,3072]{1,0:T(8,128)(2,1)S(1)} %copy-done.4, pred[]{:T(512)S(6)} %eq.48, f32[128,1,384]{2,0,1:T(8,128)S(1)} %copy.23, f32[128,1,384]{2,0,1:T(8,128)S(1)} %copy.24), kind=kOutput, calls=%fused_computation | convolution fusion | flops 304840704 | bytes 4326913 | tf_op jit(solution)/shard_map/dot_general | solution.py:437
  9.1 98.7 %experts.1 = (bf16[2,128,3072]{2,1,0:T(8,128)(2,1)}, bf16[3072,256]{1,0:T(8,128)(2,1)}, bf16[3072,256]{1,0:T(8,128)(2,1)}, bf16[256,3072]{1,0:T(8,128)(2,1)}) custom-call(bf16[2,192,3072]{2,1,0:T(8,128)(2,1)} %bitcast.19, bf16[128,384]{1,0:T(8,128)(2,1)} %get-tuple-element.18.first_pick, bf16[128,384]{1,0:T(8,128)(2,1)} %get-tuple-element.17.second_pick, ...), custom_call_target="tpu_custom_call" | custom-call | tf_op jit(solution)/shard_map/experts/pallas_call | solution.py:443
  107.8 0.0 copy-start.2
  107.8 2.7 %slice_bitcast_fusion = (bf16[128,3072]{1,0:T(8,128)(2,1)}, bf16[128,3072]{1,0:T(8,128)(2,1)}) fusion(bf16[2,128,3072]{2,1,0:T(8,128)(2,1)} %get-tuple-element.9), kind=kLoop, calls=%fused_computation.1 | loop fusion | bytes 3145728 | tf_op jit(solution)/shard_map/squeeze | solution.py:484
  110.5 0.0 copy-done.2
  110.5 0.0 copy-start.1
  110.5 1.1 copy.28
  111.7 0.8 copy-done.1
  112.5 0.0 copy-start
  112.5 1.1 copy.29
  113.7 0.8 copy-done
  114.5 1.1 copy.30
  (7 shorter events, 0.1 us)
Async XLA Ops:
  2.5 4.3 %copy-start.3 = (bf16[128,3072]{1,0:T(8,128)(2,1)S(1)}, bf16[128,3072]{1,0:T(8,128)(2,1)}, u32[]{:S(2)}) copy-start(bf16[128,3072]{1,0:T(8,128)(2,1)} %param.7) | copy-start | bytes 2359300
  2.5 4.3 %copy-start.4 = (bf16[128,3072]{1,0:T(8,128)(2,1)S(1)}, bf16[128,3072]{1,0:T(8,128)(2,1)}, u32[]{:S(2)}) copy-start(bf16[128,3072]{1,0:T(8,128)(2,1)} %param.8) | copy-start | bytes 2359300
  107.8 2.7 %copy-start.2 = (bf16[3072,256]{1,0:T(8,128)(2,1)S(1)}, bf16[3072,256]{1,0:T(8,128)(2,1)}, u32[]{:S(2)}) copy-start(bf16[3072,256]{1,0:T(8,128)(2,1)} %get-tuple-element.10) | copy-start | bytes 4718596
  110.5 2.0 %copy-start.1 = (bf16[3072,256]{1,0:T(8,128)(2,1)S(1)}, bf16[3072,256]{1,0:T(8,128)(2,1)}, u32[]{:S(2)}) copy-start(bf16[3072,256]{1,0:T(8,128)(2,1)} %get-tuple-element.11) | copy-start | bytes 4718596
  112.5 2.0 %copy-start = (bf16[256,3072]{1,0:T(8,128)(2,1)S(1)}, bf16[256,3072]{1,0:T(8,128)(2,1)}, u32[]{:S(2)}) copy-start(bf16[256,3072]{1,0:T(8,128)(2,1)} %get-tuple-element.12) | copy-start | bytes 4718596

commit v2 on v1

v2 whole, which is shorter than its diff:
```python
import functools

import jax
import jax.numpy as jnp
from jax import lax
from jax.experimental import pallas as pl
from jax.experimental.pallas import tpu as pltpu
from jax.sharding import PartitionSpec as P

MESH = pl.DeviceIdType.MESH
NY, NZH, NZ, NX, NC = 4, 2, 4, 4, 2
BF, F32 = jnp.bfloat16, jnp.float32
TRAIL = (((1,), (1,)), ((), ()))
LEAD = (((0,), (0,)), ((), ()))


class Dims:
    def __init__(self, tok, feat, hid):
        self.tok, self.feat, self.hid = tok, feat, hid
        self.cap = tok * 3 // 8
        self.grp = NY * self.cap
        self.quart = feat // NX
        self.half = self.quart // 2
        self.tile = self.quart // 6


def experts_kernel(
    dims,
    routes, weights, tokens_hbm, cotangent_hbm, gate_hbm, up_hbm, down_hbm,
    out_hbm, dx_hbm, sx_hbm, sdy_hbm, hid_hbm, gdy_hbm, udy_hbm,
    mine, first, second, send,
    arr, wg, wu, wd, hid, gdy, udy, tt, dd, rl1, rr1, rl2, rr2, yy, zr, ww, uu, outs,
    ss, rs, ls,
):
    scope = jax.named_scope
    cap, grp, quart, half, tile = dims.cap, dims.grp, dims.quart, dims.half, dims.tile
    dp, fs = lax.axis_index("dp"), lax.axis_index("fsdp")
    y, zh = dp // 2, dp % 2
    z, x, k = fs // 8, (fs // 2) % 4, fs % 2
    other = 1 - k

    def dev(yy_, zh_, z_, x_, k_):
        return (yy_ * 2 + zh_, (z_ * 4 + x_) * 2 + k_)

    def up_y(d):
        return (y + d) % 4

    right, left = dev(y, zh, z, (x + 1) % 4, k), dev(y, zh, z, (x + 3) % 4, k)
    sibling = dev(y, zh, z, x, other)

    used = [0]
    pending = []

    def fresh():
        used[0] += 1
        return used[0] - 1

    def copy(i, src, dst, to):
        return pltpu.make_async_remote_copy(
            src_ref=src, dst_ref=dst, send_sem=ss.at[i], recv_sem=rs.at[i],
            device_id=to, device_id_type=MESH,
        )

    def push(i, src, dst, to):
        c = copy(i, src, dst, to)
        c.start()
        pending.append(c)

    def got(i, region):
        copy(i, region, region, sibling).wait_recv()

    def qcols(q, off=0, width=None):
        return pl.ds(pl.multiple_of(q * quart + off, 128), quart if width is None else width)

    def rows_of(b):
        return pl.ds(pl.multiple_of(b * cap, 16), cap)

    def tcols(t, base=0):
        return pl.ds(pl.multiple_of(base + t * tile, 128), tile)

    barrier = pltpu.get_barrier_semaphore()
    partners = [right, left, sibling]
    for d in range(1, 4):
        partners.append(dev(y, zh, (z + d) % 4, x, k))
    for d in range(4):
        if d:
            partners.append(dev(up_y(d), zh, z, x, k))
        partners.append(dev(up_y(d), 1 - zh, z, x, k))
    for p in partners:
        pl.semaphore_signal(barrier, inc=1, device_id=p, device_id_type=MESH)

    @pl.when(k == 0)
    def _():
        pltpu.make_async_copy(tokens_hbm, mine, ls.at[3]).start()

    @pl.when(k == 1)
    def _():
        pltpu.make_async_copy(cotangent_hbm, mine, ls.at[3]).start()

    loads = [
        pltpu.make_async_copy(s, d, ls.at[n])
        for n, (s, d) in enumerate(((gate_hbm, wg), (up_hbm, wu), (down_hbm, wd)))
    ]
    for c in loads:
        c.start()

    experts = NY * NZH
    seat = lax.broadcasted_iota(jnp.int32, (experts, dims.tok), 0)
    expert = (seat % NY) * NZH + seat // NY
    hit_first = (routes[0:1, :] == expert).astype(F32)
    hit_second = (routes[1:2, :] == expert).astype(F32)
    earlier = (
        lax.broadcasted_iota(jnp.int32, (dims.tok, dims.tok), 0)
        < lax.broadcasted_iota(jnp.int32, (dims.tok, dims.tok), 1)
    ).astype(F32).astype(BF)
    place = jnp.dot(
        (hit_first + hit_second).astype(BF), earlier, preferred_element_type=F32
    )
    slot = lax.broadcasted_iota(jnp.int32, (cap, dims.tok), 0).astype(F32)
    for e in range(experts):
        here = (place[e : e + 1, :] == slot).astype(F32)
        at = pl.ds((e % NY) * cap, cap)
        first[e // NY, at] = (here * hit_first[e : e + 1, :]).astype(BF)
        second[e // NY, at] = (here * hit_second[e : e + 1, :]).astype(BF)

    def fill(g, at):
        f, s = first[g].astype(F32), second[g].astype(F32)
        scale = jnp.sum(f * weights[0:1, :] + s * weights[1:2, :], axis=1, keepdims=True)
        scale = jnp.where(k == 0, jnp.ones_like(scale), scale)
        send[g, :, at] = (
            jnp.dot((f + s).astype(BF), mine[:, at], preferred_element_type=F32) * scale
        ).astype(BF)

    zc = 1 - zh
    pltpu.make_async_copy(tokens_hbm, mine, ls.at[3]).wait()
    with scope("fill_cross"):
        fill(zc, qcols(x))
    with scope("barrier"):
        pl.semaphore_wait(barrier, len(partners))
    ring_order = [(0, 2), (1, 0), (1, 1), (1, 3), (1, 2)]
    send_ids = {(g, d): fresh() for g in range(2) for d in range(4)}
    both_ids = {(g, d): fresh() for g in range(2) for d in range(4)}
    ring = {b: [fresh() for _ in range(4)] for b in ring_order}
    for d in (0, 1, 3, 2):
        push(
            send_ids[1, d],
            send.at[zc, rows_of(up_y(d)), qcols(x)],
            arr.at[k, zh, rows_of(y), qcols(x)],
            dev(up_y(d), zc, z, x, k),
        )
    with scope("fill_same"):
        for q in (x, (x + 1) % 4, (x + 2) % 4, (x + 3) % 4):
            fill(zh, qcols(q))
    push(
        send_ids[0, 2],
        send.at[zh, rows_of(up_y(2)), qcols(x)],
        arr.at[k, zh, rows_of(y), qcols(x)],
        dev(up_y(2), zh, z, x, k),
    )
    for d in (1, 3):
        push(
            send_ids[0, d],
            send.at[zh, rows_of(up_y(d))],
            arr.at[k, zh, rows_of(y)],
            dev(up_y(d), zh, z, x, k),
        )
    push(both_ids[0, 0], send.at[zh, rows_of(y)], arr.at[k, zh, rows_of(y)], sibling)
    arr[k, zh, rows_of(y)] = send[zh, rows_of(y)]

    def block_of(b, *cols):
        g, d = b
        rows = rows_of(up_y(4 - d) if d else y)
        return arr.at[(k, zc if g else zh, rows) + cols]

    def ring_one(b):
        with scope(f"ring_one_{b[0]}{b[1]}"):
            near = block_of(b, qcols(x))
            got(send_ids[b], near)
            push(ring[b][0], near, near, right)
            push(ring[b][1], near, near, left)

    def ring_two(b):
        with scope(f"ring_two_{b[0]}{b[1]}"):
            got(ring[b][0], block_of(b, qcols((x + 3) % 4)))
            near = block_of(b, qcols((x + 3) % 4, 0, half))
            push(ring[b][2], near, near, right)
            got(ring[b][1], block_of(b, qcols((x + 1) % 4)))
            near = block_of(b, qcols((x + 1) % 4, half, half))
            push(ring[b][3], near, near, left)

    def ring_end(b):
        with scope(f"ring_end_{b[0]}{b[1]}"):
            got(ring[b][2], block_of(b, qcols((x + 2) % 4, 0, half)))
            got(ring[b][3], block_of(b, qcols((x + 2) % 4, half, half)))
            push(both_ids[b], block_of(b), block_of(b), sibling)

    def same_block(d):
        with scope(f"same_block_{d}"):
            got(send_ids[0, d], block_of((0, d)))
            push(both_ids[0, d], block_of((0, d)), block_of((0, d)), sibling)

    def both_here(g):
        with scope(f"both_here_{g}"):
            for d in range(4):
                rows = rows_of(up_y(4 - d) if d else y)
                got(both_ids[g, d], arr.at[other, zc if g else zh, rows])

    def first_stage(g):
        zg = zh if g == 0 else zc
        gate_pre = jnp.dot(arr[0, zg], wg[...], preferred_element_type=F32)
        up_pre = jnp.dot(arr[0, zg], wu[...], preferred_element_type=F32)
        hidden_dy = lax.dot_general(arr[1, zg], wd[...], TRAIL, preferred_element_type=F32)
        sigma = jax.nn.sigmoid(gate_pre)
        active = gate_pre * sigma
        hid[zg] = (active * up_pre).astype(BF)
        gdy[zg] = (hidden_dy * up_pre * sigma * (1.0 + gate_pre * (1.0 - sigma))).astype(BF)
        udy[zg] = (hidden_dy * active).astype(BF)

    quarters = [(x + 2) % 4, (x + 1) % 4, (x + 3) % 4, x]
    swap_ids = {(g, n): fresh() for g in range(2) for n in range(4)}

    hop_ids = {(g, n): fresh() for g in range(2) for n in range(6)}

    def plus(a, b):
        return (a.astype(F32) + b.astype(F32)).astype(BF)

    def chip_sum(g, n):
        q = quarters[n]
        got(swap_ids[g, n], dd.at[g, :, qcols(q)])
        tt[g, k, :, qcols(q)] = plus(tt[g, k, :, qcols(q)], dd[g, :, qcols(q)])
        if n == 0:
            push(hop_ids[g, 0], tt.at[g, k, :, qcols(q, 0, half)], rl1.at[g], right)
            push(hop_ids[g, 1], tt.at[g, k, :, qcols(q, half, half)], rr1.at[g], left)
        if n == 1:
            push(
                hop_ids[g, 2], tt.at[g, k, :, qcols(q, half, half)],
                rl2.at[g, :, pl.ds(half, half)], right,
            )
        if n == 2:
            push(
                hop_ids[g, 3], tt.at[g, k, :, qcols(q, 0, half)],
                rr2.at[g, :, pl.ds(0, half)], left,
            )

    def second_stage(g):
        zg = zh if g == 0 else zc
        width = quart // 3
        for n, q in enumerate(quarters):

            def body(c, carry, q=q):
                at = pl.ds(pl.multiple_of(q * quart + c * width, 128), width)
                tt[g, 0, :, at] = jnp.dot(
                    hid[zg], wd[:, at], preferred_element_type=F32
                ).astype(BF)
                tt[g, 1, :, at] = (
                    lax.dot_general(gdy[zg], wg[at, :], TRAIL, preferred_element_type=F32)
                    + lax.dot_general(udy[zg], wu[at, :], TRAIL, preferred_element_type=F32)
                ).astype(BF)
                return carry

            with scope(f"second_{g}{n}"):
                lax.fori_loop(0, 3, body, 0)
            push(swap_ids[g, n], tt.at[g, other, :, qcols(q)], dd.at[g, :, qcols(q)], sibling)
            if n:
                with scope(f"chip_sum_{g}{n - 1}"):
                    chip_sum(g, n - 1)

    def hop_two(g):
        got(hop_ids[g, 0], rl1.at[g])
        at = qcols(quarters[1], 0, half)
        tt[g, k, :, at] = plus(tt[g, k, :, at], rl1[g])
        push(hop_ids[g, 4], tt.at[g, k, :, at], rl2.at[g, :, pl.ds(0, half)], right)
        got(hop_ids[g, 1], rr1.at[g])
        at = qcols(quarters[2], half, half)
        tt[g, k, :, at] = plus(tt[g, k, :, at], rr1[g])
        push(hop_ids[g, 5], tt.at[g, k, :, at], rr2.at[g, :, pl.ds(half, half)], left)

    def head(zz):
        return (3 * zz + 1 - k) // 2

    def pair(zz):
        return (zz + k) % 2 == 0

    tile_ids = {(g, d, s): fresh() for g in range(2) for d in range(1, 4) for s in range(2)}

    def along_z(g):
        chip_sum(g, 3)
        for n in (2, 3, 4, 5):
            region = (rl2 if n in (2, 4) else rr2).at[
                g, :, pl.ds(half if n in (2, 5) else 0, half)
            ]
            got(hop_ids[g, n], region)
        yy[g] = (
            tt[g, k, :, qcols(x)].astype(F32) + rl2[g].astype(F32) + rr2[g].astype(F32)
        ).astype(BF)
        for d in range(1, 4):
            zz = (z + d) % 4
            to = dev(y, zh, zz, x, k)
            push(tile_ids[g, d, 0], yy.at[g, :, tcols(head(zz))], zr.at[g, d - 1, 0], to)

            @pl.when(pair(zz))
            def _(d=d, zz=zz, to=to):
                copy(
                    tile_ids[g, d, 1], yy.at[g, :, tcols(head(zz) + 1)], zr.at[g, d - 1, 1], to
                ).start()

    back_ids = {(g, d): fresh() for g in range(2) for d in range(4)}

    def home(g):
        zg = zh if g == 0 else zc

        def summed(s):
            total = yy[g, :, tcols(head(z) + s)].astype(F32)
            for d in range(1, 4):
                total = total + zr[g, d - 1, s].astype(F32)
            ww[g, :, pl.ds(s * tile, tile)] = total.astype(BF)

        for d in range(1, 4):
            got(tile_ids[g, d, 0], zr.at[g, d - 1, 0])
        summed(0)

        @pl.when(pair(z))
        def _():
            for d in range(1, 4):
                got(tile_ids[g, d, 1], zr.at[g, d - 1, 1])
            summed(1)

        @pl.when(jnp.logical_not(pair(z)))
        def _():
            ww[g, :, pl.ds(tile, tile)] = jnp.zeros((grp, tile), BF)

        for d in (1, 3, 2, 0):
            if g == 0 and d == 0:
                uu[zh, rows_of(y)] = ww[0, rows_of(y)]
            else:
                push(
                    back_ids[g, d], ww.at[g, rows_of(up_y(d))], uu.at[zh, rows_of(y)],
                    dev(up_y(d), zg, z, x, k),
                )

    for b in ring_order:
        ring_one(b)
    for d in (1, 3):
        same_block(d)
    for b in ring_order:
        ring_two(b)
    ring_end((0, 2))
    with scope("weights_here"):
        for c in loads:
            c.wait()
    both_here(0)
    with scope("first_0"):
        first_stage(0)
    for b in ring_order[1:]:
        ring_end(b)
    second_stage(0)
    both_here(1)
    stores = [
        pltpu.make_async_copy(s, d, ls.at[4 + n])
        for n, (s, d) in enumerate(((arr.at[0], sx_hbm), (arr.at[1], sdy_hbm)))
    ]
    with scope("first_1"):
        first_stage(1)
    stores += [
        pltpu.make_async_copy(s, d, ls.at[6 + n])
        for n, (s, d) in enumerate(((hid, hid_hbm), (gdy, gdy_hbm), (udy, udy_hbm)))
    ]
    for c in stores:
        c.start()
    with scope("hop_two_0"):
        hop_two(0)
    second_stage(1)
    with scope("along_z_0"):
        along_z(0)
    with scope("hop_two_1"):
        hop_two(1)
    with scope("home_0"):
        home(0)
    with scope("along_z_1"):
        along_z(1)
    with scope("home_1"):
        home(1)

    with scope("wait_home"):
        for g in range(2):
            zg = zh if g == 0 else zc
            for d in range(4):
                if g or d:
                    got(back_ids[g, d], uu.at[zg, rows_of(up_y(4 - d) if d else y)])
    slots = uu[...].reshape(2 * grp, 2 * tile)
    same_token = (
        lax.broadcasted_iota(jnp.int32, (dims.tok, dims.tok), 0)
        == lax.broadcasted_iota(jnp.int32, (dims.tok, dims.tok), 1)
    )
    share_first = jnp.sum(
        jnp.where(same_token, weights[0:1, :], 0.0), axis=1, keepdims=True
    )
    share_second = jnp.sum(
        jnp.where(same_token, weights[1:2, :], 0.0), axis=1, keepdims=True
    )
    share_first = jnp.where(k == 0, share_first, jnp.ones_like(share_first))
    share_second = jnp.where(k == 0, share_second, jnp.ones_like(share_second))
    mixed = (
        share_first
        * lax.dot_general(
            first[...].reshape(2 * grp, dims.tok), slots, LEAD, preferred_element_type=F32
        )
        + share_second
        * lax.dot_general(
            second[...].reshape(2 * grp, dims.tok), slots, LEAD, preferred_element_type=F32
        )
    ).astype(BF)
    base = x * quart
    outs[k, :, tcols(head(z), base)] = mixed[:, :tile]

    @pl.when(pair(z))
    def _():
        outs[k, :, tcols(head(z) + 1, base)] = mixed[:, tile:]

    last_ids = {(d, s): fresh() for d in range(1, 4) for s in range(2)}
    to_right = [fresh() for _ in range(6)][0]
    to_left = [fresh() for _ in range(6)][0]
    onward = [fresh() for _ in range(6)][0]
    swap_last = [fresh() for _ in range(4)]

    def cell(q, t):
        return outs.at[k, :, tcols(t, q * quart)]

    def each_tile(zz, action):
        action(0)
        pl.when(pair(zz))(lambda: action(1))

    def near_x(t):
        copy(to_right + t, cell(x, t), cell(x, t), right).start()
        copy(to_left + t, cell(x, t), cell(x, t), left).start()

    def first_out(s):
        t = head(z) + s
        near_x(t)
        for d in (1, 3, 2):
            to = dev(y, zh, (z + d) % 4, x, k)
            copy(last_ids[d, s], cell(x, t), cell(x, t), to).start()

    each_tile(z, first_out)
    with scope("last_z"):
        for d in (1, 3, 2):
            zz = (z + 4 - d) % 4

            def relay(s, d=d, zz=zz):
                t = head(zz) + s
                got(last_ids[d, s], cell(x, t))
                near_x(t)

            each_tile(zz, relay)
    push(swap_last[0], outs.at[k, :, qcols(x)], outs.at[k, :, qcols(x)], sibling)
    with scope("last_x"):
        for d in (0, 1, 3, 2):
            zz = (z + 4 - d) % 4

            def onwards(s, zz=zz):
                t = head(zz) + s
                from_left, from_right = cell((x + 3) % 4, t), cell((x + 1) % 4, t)
                got(to_right + t, from_left)

                @pl.when(t < 3)
                def _():
                    copy(onward + t, from_left, from_left, right).start()

                got(to_left + t, from_right)

                @pl.when(t >= 3)
                def _():
                    copy(onward + t, from_right, from_right, left).start()

            each_tile(zz, onwards)
    for n, q in ((1, (x + 3) % 4), (2, (x + 1) % 4)):
        push(swap_last[n], outs.at[k, :, qcols(q)], outs.at[k, :, qcols(q)], sibling)
    with scope("last_far"):
        for t in range(6):
            got(onward + t, cell((x + 2) % 4, t))
    far = outs.at[k, :, qcols((x + 2) % 4)]
    push(swap_last[3], far, far, sibling)
    with scope("last_swap"):
        for n, q in enumerate((x, (x + 3) % 4, (x + 1) % 4, (x + 2) % 4)):
            got(swap_last[n], outs.at[other, :, qcols(q)])
    results = [
        pltpu.make_async_copy(outs.at[n], d, ls.at[9 + n]) for n, d in enumerate((out_hbm, dx_hbm))
    ]
    for c in results:
        c.start()
    with scope("drain"):
        for c in pending:
            c.wait_send()
        for g in range(2):
            for d in range(1, 4):
                zz = (z + d) % 4

                @pl.when(pair(zz))
                def _(g=g, d=d, zz=zz):
                    copy(
                        tile_ids[g, d, 1], yy.at[g, :, tcols(head(zz) + 1)], zr.at[g, d - 1, 1],
                        sibling,
                    ).wait_send()

        def sent(s):
            mine_ = cell(x, head(z) + s)
            for d in range(1, 4):
                copy(last_ids[d, s], mine_, mine_, sibling).wait_send()

        each_tile(z, sent)
        for t in range(6):
            for i in (to_right, to_left, onward):
                copy(i + t, cell(x, t), cell(x, t), sibling).wait_send()
        for c in stores + results:
            c.wait()


def on_device(tokens, cotangent, routes, router_weight, w_gate, w_up, w_down):
    dims = Dims(tokens.shape[0], tokens.shape[1], w_gate.shape[2])
    grp, feat, hid = dims.grp, dims.feat, dims.hid
    half, quart, tile = dims.half, dims.quart, dims.tile
    vmem = pl.BlockSpec(memory_space=pltpu.VMEM)
    hbm = pl.BlockSpec(memory_space=pl.ANY)
    wide = jax.ShapeDtypeStruct((2, grp, feat), BF)
    narrow = jax.ShapeDtypeStruct((2, grp, hid), BF)
    whole = jax.ShapeDtypeStruct((dims.tok, feat), BF)
    output, input_grad, slot_x, slot_dy, hidden, gate_dy, up_dy = pl.pallas_call(
        functools.partial(experts_kernel, dims),
        out_shape=(whole, whole, wide, wide, narrow, narrow, narrow),
        in_specs=[vmem] * 2 + [hbm] * 5,
        out_specs=(hbm,) * 7,
        scratch_shapes=[
            pltpu.VMEM((dims.tok, feat), BF),
            pltpu.VMEM((2, grp, dims.tok), BF),
            pltpu.VMEM((2, grp, dims.tok), BF),
            pltpu.VMEM((2, grp, feat), BF),
            pltpu.VMEM((2, 2, grp, feat), BF),
            pltpu.VMEM((feat, hid), BF),
            pltpu.VMEM((feat, hid), BF),
            pltpu.VMEM((hid, feat), BF),
            pltpu.VMEM((2, grp, hid), BF),
            pltpu.VMEM((2, grp, hid), BF),
            pltpu.VMEM((2, grp, hid), BF),
            pltpu.VMEM((2, 2, grp, feat), BF),
            pltpu.VMEM((2, grp, feat), BF),
            pltpu.VMEM((2, grp, half), BF),
            pltpu.VMEM((2, grp, half), BF),
            pltpu.VMEM((2, grp, quart), BF),
            pltpu.VMEM((2, grp, quart), BF),
            pltpu.VMEM((2, grp, quart), BF),
            pltpu.VMEM((2, 3, 2, grp, tile), BF),
            pltpu.VMEM((2, grp, 2 * tile), BF),
            pltpu.VMEM((2, grp, 2 * tile), BF),
            pltpu.VMEM((2, dims.tok, feat), BF),
            pltpu.SemaphoreType.DMA((128,)),
            pltpu.SemaphoreType.DMA((128,)),
            pltpu.SemaphoreType.DMA((11,)),
        ],
        compiler_params=pltpu.CompilerParams(
            collective_id=0, has_side_effects=True, vmem_limit_bytes=56 * 1024 * 1024
        ),
        name="experts",
    )(routes.T, router_weight.T, tokens, cotangent, w_gate[0], w_up[0], w_down[0])
    rows = 2 * grp
    slot_x, slot_dy = slot_x.reshape(rows, feat), slot_dy.reshape(rows, feat)
    hidden, gate_dy, up_dy = (a.reshape(rows, hid) for a in (hidden, gate_dy, up_dy))

    def grad(left_rows, right_rows):
        return lax.dot_general(
            left_rows, right_rows, LEAD, preferred_element_type=F32
        ).astype(BF)[None]

    return (
        output, input_grad, grad(slot_x, gate_dy), grad(slot_x, up_dy), grad(hidden, slot_dy)
    )


def solution(mesh):
    return jax.shard_map(
        on_device,
        mesh=mesh,
        in_specs=(
            P("dp", None),
            P("dp", None),
            P("dp", None),
            P("dp", None),
            P("dp", None, "fsdp"),
            P("dp", None, "fsdp"),
            P("dp", "fsdp", None),
        ),
        out_specs=(
            P("dp", None),
            P("dp", None),
            P("dp", None, "fsdp"),
            P("dp", None, "fsdp"),
            P("dp", "fsdp", None),
        ),
        check_vma=False,
    )
```

time: 117 us -> 107 us (0.915); the launches traced: 116 us -> 107 us
  local copies, waits for them, and re-layouts: 9.22 us -> 1.78 us
  matrix products: 2.22 us -> 8.31 us
  other arithmetic: 4.76 us -> 0 us
  Pallas kernels: 98.7 us -> 96.6 us
    dot_general x1 -> x3, matrix products: 2.22 us -> 8.31 us  [grad(): lax.dot_general(left_rows, right_rows, LEAD, preferred_element_type=F32)]
    unnamed x16 -> x14, local copies, waits for them, and re-layouts: 6.15 us -> 1.78 us
    squeeze x1 -> x0, local copies, waits for them, and re-layouts: 2.73 us -> none  [on_device(): return (outs[0], outs[1], gg[None], gu[None], gd[None])]
    reduce_sum x3 -> x0, other arithmetic: 2.44 us -> none  [the longest x1 0.88 us: slot_tables(): slot_of = jnp.sum(hit_table * before[:, None, :], axis=2)]
    pallas_call x1, Pallas kernels: 98.7 us -> 96.6 us  [on_device(): pl.pallas_call(functools.partial(experts_kernel, dims), out_shape=(whole,...]
    convert_element_type x4 -> x0, other arithmetic: 1.49 us -> none  [the longest x1 0.75 us: slot_tables(): hit_table = (routes[:, :, None] == order).astype(jnp.int32)]
where the time goes in v2:
time: 107 us
  Pallas kernels  96.6 us (90%)
  matrix products  8.31 us (8%)
  local copies, waits for them, and re-layouts  1.78 us (2%)
    pallas_call x1, Pallas kernels, on_device(): pl.pallas_call(functools.partial(experts_kernel, dims), out_shape=(whole,...  96.6 us
    dot_general x3, matrix products, grad(): lax.dot_general(left_rows, right_rows, LEAD, preferred_element_type=F32)  8.31 us

profile of v2, /device:TPU:1, one launch (start us, length us, event | category | flops | bytes accessed | tf_op | source)
XLA Modules:
  0.0 107.3 jit_solution(2017565035641620421)
XLA Ops:
  0.6 96.6 %experts.1 = (bf16[128,3072]{1,0:T(8,128)(2,1)}, bf16[128,3072]{1,0:T(8,128)(2,1)}, bf16[2,192,3072]{2,1,0:T(8,128)(2,1)}, bf16[2,192,3072]{2,1,0:T(8,128)(2,1)}...) custom-call(s32[2,128]{1,0:T(2,128)} %bitcast.38, f32[2,128]{1,0:T(2,128)} %bitcast.39, ...), custom_call_target="tpu_custom_call" | custom-call | tf_op jit(solution)/shard_map/experts/pallas_call | solution.py:527
  97.2 0.0 copy-start.4
  97.2 0.0 copy-start.5
  97.2 4.0 %fusion.5 = bf16[1,3072,256]{2,1,0:T(8,128)(2,1)} fusion(bf16[2,192,3072]{2,1,0:T(8,128)(2,1)} %get-tuple-element.14, bf16[2,192,256]{2,1,0:T(8,128)(2,1)} %get-tuple-element.15), kind=kOutput, calls=%fused_computation.8 | convolution fusion | flops 604766208 | bytes 4128768 | tf_op jit(solution)/shard_map/dot_general | solution.py:569
  101.2 0.0 copy-done.4
  101.2 0.0 copy-done.5
  101.2 0.0 copy-start
  101.2 0.0 copy-start.3
  101.2 2.2 %fusion.4 = bf16[1,3072,256]{2,1,0:T(8,128)(2,1)} fusion(bf16[2,192,3072]{2,1,0:T(8,128)(2,1)S(1)} %copy-done.4, bf16[2,192,256]{2,1,0:T(8,128)(2,1)S(1)} %copy-done.5), kind=kOutput, calls=%fused_computation.7 | convolution fusion | flops 604766208 | bytes 4128768 | tf_op jit(solution)/shard_map/dot_general | solution.py:569
  103.4 0.0 copy-done
  103.4 0.0 copy-done.3
  103.4 0.0 copy-start.2
  103.4 0.0 copy-start.1
  103.4 2.2 %fusion.3 = bf16[1,256,3072]{2,1,0:T(8,128)(2,1)} fusion(bf16[2,192,256]{2,1,0:T(8,128)(2,1)S(1)} %copy-done.3, bf16[2,192,3072]{2,1,0:T(8,128)(2,1)S(1)} %copy-done), kind=kOutput, calls=%fused_computation.6 | convolution fusion | flops 604766208 | bytes 4128768 | tf_op jit(solution)/shard_map/dot_general | solution.py:569
  105.6 0.0 copy-done.2
  105.6 0.9 copy.14
  106.5 0.0 copy-done.1
  106.5 0.9 copy.15
Async XLA Ops:
  97.2 4.0 %copy-start.4 = (bf16[2,192,3072]{2,1,0:T(8,128)(2,1)S(1)}, bf16[2,192,3072]{2,1,0:T(8,128)(2,1)}, u32[]{:S(2)}) copy-start(bf16[2,192,3072]{2,1,0:T(8,128)(2,1)} %get-tuple-element.14) | copy-start | bytes 7077892
  97.2 4.0 %copy-start.5 = (bf16[2,192,256]{2,1,0:T(8,128)(2,1)S(1)}, bf16[2,192,256]{2,1,0:T(8,128)(2,1)}, u32[]{:S(2)}) copy-start(bf16[2,192,256]{2,1,0:T(8,128)(2,1)} %get-tuple-element.16) | copy-start | bytes 589828
  101.2 2.2 %copy-start = (bf16[2,192,3072]{2,1,0:T(8,128)(2,1)S(1)}, bf16[2,192,3072]{2,1,0:T(8,128)(2,1)}, u32[]{:S(2)}) copy-start(bf16[2,192,3072]{2,1,0:T(8,128)(2,1)} %get-tuple-element.18) | copy-start | bytes 7077892
  101.2 2.2 %copy-start.3 = (bf16[2,192,256]{2,1,0:T(8,128)(2,1)S(1)}, bf16[2,192,256]{2,1,0:T(8,128)(2,1)}, u32[]{:S(2)}) copy-start(bf16[2,192,256]{2,1,0:T(8,128)(2,1)} %get-tuple-element.17) | copy-start | bytes 589828
  103.4 2.2 %copy-start.2 = (bf16[128,3072]{1,0:T(8,128)(2,1)S(1)}, bf16[128,3072]{1,0:T(8,128)(2,1)}, u32[]{:S(2)}) copy-start(bf16[128,3072]{1,0:T(8,128)(2,1)} %get-tuple-element.24) | copy-start | bytes 2359300
  103.4 3.0 %copy-start.1 = (bf16[128,3072]{1,0:T(8,128)(2,1)S(1)}, bf16[128,3072]{1,0:T(8,128)(2,1)}, u32[]{:S(2)}) copy-start(bf16[128,3072]{1,0:T(8,128)(2,1)} %get-tuple-element.25) | copy-start | bytes 2359300

commit v3 on v2

--- a/solution.py
+++ b/solution.py
@@ -27,9 +27,9 @@
 def experts_kernel(
     dims,
     routes, weights, tokens_hbm, cotangent_hbm, gate_hbm, up_hbm, down_hbm,
-    out_hbm, dx_hbm, sx_hbm, sdy_hbm, hid_hbm, gdy_hbm, udy_hbm,
+    outs, gg, gu, gd,
     mine, first, second, send,
-    arr, wg, wu, wd, hid, gdy, udy, tt, dd, rl1, rr1, rl2, rr2, yy, zr, ww, uu, outs,
+    arr, wg, wu, wd, hid, gdy, udy, tt, dd, rl1, rr1, rl2, rr2, yy, uu,
     ss, rs, ls,
 ):
     scope = jax.named_scope
@@ -80,12 +80,11 @@
 
     barrier = pltpu.get_barrier_semaphore()
     partners = [right, left, sibling]
-    for d in range(1, 4):
-        partners.append(dev(y, zh, (z + d) % 4, x, k))
     for d in range(4):
-        if d:
-            partners.append(dev(up_y(d), zh, z, x, k))
-        partners.append(dev(up_y(d), 1 - zh, z, x, k))
+        for turn in range(4):
+            if d or turn:
+                partners.append(dev(up_y(d), zh, (z + turn) % 4, x, k))
+            partners.append(dev(up_y(d), 1 - zh, (z + turn) % 4, x, k))
     for p in partners:
         pl.semaphore_signal(barrier, inc=1, device_id=p, device_id_type=MESH)
 
@@ -219,61 +218,69 @@
     quarters = [(x + 2) % 4, (x + 1) % 4, (x + 3) % 4, x]
     swap_ids = {(g, n): fresh() for g in range(2) for n in range(4)}
 
-    hop_ids = {(g, n): fresh() for g in range(2) for n in range(6)}
+    hop_ids = {(g, h, n): fresh() for g in range(2) for h in range(2) for n in range(6)}
+    part = grp // 2
 
     def plus(a, b):
         return (a.astype(F32) + b.astype(F32)).astype(BF)
 
+    def rows_h(h):
+        return pl.ds(h * part, part)
+
+    def hop(g, h, n):
+        q = quarters[(0, 0, 1, 2, 1, 2)[n]]
+        off = (0, half, half, 0, 0, half)[n]
+        rows = rows_h(h)
+        source = tt.at[g, k, rows, qcols(q, off, half)]
+        if n < 2:
+            target = (rl1, rr1)[n].at[g, rows]
+        else:
+            target = (rl2 if n % 2 == 0 else rr2).at[g, rows, pl.ds(off, half)]
+        push(hop_ids[g, h, n], source, target, right if n % 2 == 0 else left)
+
     def chip_sum(g, n):
-        q = quarters[n]
-        got(swap_ids[g, n], dd.at[g, :, qcols(q)])
-        tt[g, k, :, qcols(q)] = plus(tt[g, k, :, qcols(q)], dd[g, :, qcols(q)])
-        if n == 0:
-            push(hop_ids[g, 0], tt.at[g, k, :, qcols(q, 0, half)], rl1.at[g], right)
-            push(hop_ids[g, 1], tt.at[g, k, :, qcols(q, half, half)], rr1.at[g], left)
-        if n == 1:
-            push(
-                hop_ids[g, 2], tt.at[g, k, :, qcols(q, half, half)],
-                rl2.at[g, :, pl.ds(half, half)], right,
-            )
-        if n == 2:
-            push(
-                hop_ids[g, 3], tt.at[g, k, :, qcols(q, 0, half)],
-                rr2.at[g, :, pl.ds(0, half)], left,
-            )
-
-    def second_stage(g):
+        with scope(f"chip_sum_{g}{n}"):
+            q = quarters[n]
+            got(swap_ids[g, n], dd.at[g, :, qcols(q)])
+            tt[g, k, :, qcols(q)] = plus(tt[g, k, :, qcols(q)], dd[g, :, qcols(q)])
+            if n == 0:
+                for h in range(2):
+                    hop(g, h, 0)
+                    hop(g, h, 1)
+            if n in (1, 2):
+                hop(g, 0, n + 1)
+
+    def second_part(g, n):
         zg = zh if g == 0 else zc
         width = quart // 3
-        for n, q in enumerate(quarters):
-
-            def body(c, carry, q=q):
-                at = pl.ds(pl.multiple_of(q * quart + c * width, 128), width)
-                tt[g, 0, :, at] = jnp.dot(
-                    hid[zg], wd[:, at], preferred_element_type=F32
-                ).astype(BF)
-                tt[g, 1, :, at] = (
-                    lax.dot_general(gdy[zg], wg[at, :], TRAIL, preferred_element_type=F32)
-                    + lax.dot_general(udy[zg], wu[at, :], TRAIL, preferred_element_type=F32)
-                ).astype(BF)
-                return carry
-
-            with scope(f"second_{g}{n}"):
-                lax.fori_loop(0, 3, body, 0)
-            push(swap_ids[g, n], tt.at[g, other, :, qcols(q)], dd.at[g, :, qcols(q)], sibling)
-            if n:
-                with scope(f"chip_sum_{g}{n - 1}"):
-                    chip_sum(g, n - 1)
-
-    def hop_two(g):
-        got(hop_ids[g, 0], rl1.at[g])
-        at = qcols(quarters[1], 0, half)
-        tt[g, k, :, at] = plus(tt[g, k, :, at], rl1[g])
-        push(hop_ids[g, 4], tt.at[g, k, :, at], rl2.at[g, :, pl.ds(0, half)], right)
-        got(hop_ids[g, 1], rr1.at[g])
-        at = qcols(quarters[2], half, half)
-        tt[g, k, :, at] = plus(tt[g, k, :, at], rr1[g])
-        push(hop_ids[g, 5], tt.at[g, k, :, at], rr2.at[g, :, pl.ds(half, half)], left)
+        q = quarters[n]
+
+        def body(c, carry):
+            at = pl.ds(pl.multiple_of(q * quart + c * width, 128), width)
+            tt[g, 0, :, at] = jnp.dot(
+                hid[zg], wd[:, at], preferred_element_type=F32
+            ).astype(BF)
+            tt[g, 1, :, at] = (
+                lax.dot_general(gdy[zg], wg[at, :], TRAIL, preferred_element_type=F32)
+                + lax.dot_general(udy[zg], wu[at, :], TRAIL, preferred_element_type=F32)
+            ).astype(BF)
+            return carry
+
+        with scope(f"second_{g}{n}"):
+            lax.fori_loop(0, 3, body, 0)
+        push(swap_ids[g, n], tt.at[g, other, :, qcols(q)], dd.at[g, :, qcols(q)], sibling)
+
+    def hop_two(g, h):
+        with scope(f"hop_two_{g}{h}"):
+            rows = rows_h(h)
+            got(hop_ids[g, h, 0], rl1.at[g, rows])
+            at = qcols(quarters[1], 0, half)
+            tt[g, k, rows, at] = plus(tt[g, k, rows, at], rl1[g, rows])
+            hop(g, h, 4)
+            got(hop_ids[g, h, 1], rr1.at[g, rows])
+            at = qcols(quarters[2], half, half)
+            tt[g, k, rows, at] = plus(tt[g, k, rows, at], rr1[g, rows])
+            hop(g, h, 5)
 
     def head(zz):
         return (3 * zz + 1 - k) // 2
@@ -281,113 +288,170 @@
     def pair(zz):
         return (zz + k) % 2 == 0
 
-    tile_ids = {(g, d, s): fresh() for g in range(2) for d in range(1, 4) for s in range(2)}
-
-    def along_z(g):
-        chip_sum(g, 3)
-        for n in (2, 3, 4, 5):
-            region = (rl2 if n in (2, 4) else rr2).at[
-                g, :, pl.ds(half if n in (2, 5) else 0, half)
-            ]
-            got(hop_ids[g, n], region)
-        yy[g] = (
-            tt[g, k, :, qcols(x)].astype(F32) + rl2[g].astype(F32) + rr2[g].astype(F32)
-        ).astype(BF)
-        for d in range(1, 4):
+    home_ids = {(g, d): [fresh() for _ in range(NY)][0] for g in range(2) for d in range(4)}
+
+    def home_copy(g, d, b, wide):
+        width = 2 * tile if wide else tile
+        zz = (z + d) % 4
+        return pltpu.make_async_remote_copy(
+            src_ref=yy.at[g, rows_of(b), pl.ds(pl.multiple_of(head(zz) * tile, 128), width)],
+            dst_ref=uu.at[zh, d, rows_of(y), pl.ds(0, width)],
+            send_sem=ss.at[home_ids[g, d] + b], recv_sem=rs.at[home_ids[g, d] + y],
+            device_id=dev(b, zh if g == 0 else zc, zz, x, k), device_id_type=MESH,
+        )
+
+    def by_width(zz, action):
+        pl.when(pair(zz))(lambda: action(True))
+        pl.when(jnp.logical_not(pair(zz)))(lambda: action(False))
+
+    def each_home(g, b, action):
+        for d in (1, 3, 2, 0):
             zz = (z + d) % 4
-            to = dev(y, zh, zz, x, k)
-            push(tile_ids[g, d, 0], yy.at[g, :, tcols(head(zz))], zr.at[g, d - 1, 0], to)
-
-            @pl.when(pair(zz))
-            def _(d=d, zz=zz, to=to):
-                copy(
-                    tile_ids[g, d, 1], yy.at[g, :, tcols(head(zz) + 1)], zr.at[g, d - 1, 1], to
-                ).start()
-
-    back_ids = {(g, d): fresh() for g in range(2) for d in range(4)}
-
-    def home(g):
-        zg = zh if g == 0 else zc
-
-        def summed(s):
-            total = yy[g, :, tcols(head(z) + s)].astype(F32)
-            for d in range(1, 4):
-                total = total + zr[g, d - 1, s].astype(F32)
-            ww[g, :, pl.ds(s * tile, tile)] = total.astype(BF)
-
-        for d in range(1, 4):
-            got(tile_ids[g, d, 0], zr.at[g, d - 1, 0])
-        summed(0)
-
-        @pl.when(pair(z))
-        def _():
-            for d in range(1, 4):
-                got(tile_ids[g, d, 1], zr.at[g, d - 1, 1])
-            summed(1)
-
-        @pl.when(jnp.logical_not(pair(z)))
-        def _():
-            ww[g, :, pl.ds(tile, tile)] = jnp.zeros((grp, tile), BF)
-
-        for d in (1, 3, 2, 0):
             if g == 0 and d == 0:
-                uu[zh, rows_of(y)] = ww[0, rows_of(y)]
+                pl.when(b != y)(
+                    lambda d=d, zz=zz: by_width(zz, lambda wide: action(home_copy(g, d, b, wide)))
+                )
             else:
-                push(
-                    back_ids[g, d], ww.at[g, rows_of(up_y(d))], uu.at[zh, rows_of(y)],
-                    dev(up_y(d), zg, z, x, k),
+                by_width(zz, lambda wide, d=d: action(home_copy(g, d, b, wide)))
+
+    def finish(g, h):
+        with scope(f"finish_{g}{h}"):
+            rows = rows_h(h)
+            for n in (2, 3, 4, 5):
+                got(
+                    hop_ids[g, h, n],
+                    (rl2 if n % 2 == 0 else rr2).at[
+                        g, rows, pl.ds((0, half, half, 0, 0, half)[n], half)
+                    ],
                 )
-
-    for b in ring_order:
-        ring_one(b)
-    for d in (1, 3):
-        same_block(d)
-    for b in ring_order:
-        ring_two(b)
+            yy[g, rows] = (
+                tt[g, k, rows, qcols(x)].astype(F32)
+                + rl2[g, rows].astype(F32)
+                + rr2[g, rows].astype(F32)
+            ).astype(BF)
+            for b in (2 * h, 2 * h + 1):
+                each_home(g, b, lambda c: c.start())
+                if g == 0:
+
+                    @pl.when(b == y)
+                    def _(b=b):
+                        def keep(wide):
+                            for s in range(2 if wide else 1):
+                                uu[zh, 0, rows_of(y), pl.ds(s * tile, tile)] = yy[
+                                    0, rows_of(b), tcols(head(z) + s)
+                                ]
+
+                        by_width(z, keep)
+
+    def wait_home():
+        def arrived(wide):
+            width = 2 * tile if wide else tile
+            for g in range(2):
+                for d in range(4):
+                    for b in range(NY):
+                        region = uu.at[zc if g else zh, d, rows_of(b), pl.ds(0, width)]
+                        wait = pltpu.make_async_remote_copy(
+                            src_ref=region, dst_ref=region, send_sem=ss.at[home_ids[g, d] + b],
+                            recv_sem=rs.at[home_ids[g, d] + b], device_id=sibling,
+                            device_id_type=MESH,
+                        )
+                        if g == 0 and d == 0:
+                            pl.when(b != y)(wait.wait_recv)
+                        else:
+                            wait.wait_recv()
+
+        by_width(z, arrived)
+
+    def weight_grads(begin, end):
+        width = 256
+        rows = 2 * grp
+
+        def body(c, carry):
+            at = pl.ds(pl.multiple_of(c * width, 128), width)
+            xs = arr[0, :, :, at].reshape(rows, width)
+            ys = arr[1, :, :, at].reshape(rows, width)
+            gg[at, :] = lax.dot_general(
+                xs, gdy[...].reshape(rows, dims.hid), LEAD, preferred_element_type=F32
+            ).astype(BF)
+            gu[at, :] = lax.dot_general(
+                xs, udy[...].reshape(rows, dims.hid), LEAD, preferred_element_type=F32
+            ).astype(BF)
+            gd[:, at] = lax.dot_general(
+                hid[...].reshape(rows, dims.hid), ys, LEAD, preferred_element_type=F32
+            ).astype(BF)
+            return carry
+
+        with scope(f"weight_grads_{begin}"):
+            lax.fori_loop(begin, end, body, 0)
+
+    ring_one((0, 2))
+    ring_one((1, 0))
+    ring_two((0, 2))
+    ring_one((1, 1))
     ring_end((0, 2))
+    same_block(1)
+    same_block(3)
+    ring_one((1, 3))
+    ring_two((1, 0))
+    ring_one((1, 2))
+    ring_two((1, 1))
     with scope("weights_here"):
         for c in loads:
             c.wait()
     both_here(0)
     with scope("first_0"):
         first_stage(0)
-    for b in ring_order[1:]:
-        ring_end(b)
-    second_stage(0)
+    ring_end((1, 0))
+    ring_two((1, 3))
+    second_part(0, 0)
+    ring_two((1, 2))
+    ring_end((1, 1))
+    second_part(0, 1)
+    chip_sum(0, 0)
+    ring_end((1, 3))
+    second_part(0, 2)
+    chip_sum(0, 1)
+    second_part(0, 3)
+    chip_sum(0, 2)
+    ring_end((1, 2))
+    hop_two(0, 0)
+    hop(0, 1, 2)
+    hop(0, 1, 3)
     both_here(1)
-    stores = [
-        pltpu.make_async_copy(s, d, ls.at[4 + n])
-        for n, (s, d) in enumerate(((arr.at[0], sx_hbm), (arr.at[1], sdy_hbm)))
-    ]
     with scope("first_1"):
         first_stage(1)
-    stores += [
-        pltpu.make_async_copy(s, d, ls.at[6 + n])
-        for n, (s, d) in enumerate(((hid, hid_hbm), (gdy, gdy_hbm), (udy, udy_hbm)))
-    ]
-    for c in stores:
-        c.start()
-    with scope("hop_two_0"):
-        hop_two(0)
-    second_stage(1)
-    with scope("along_z_0"):
-        along_z(0)
-    with scope("hop_two_1"):
-        hop_two(1)
-    with scope("home_0"):
-        home(0)
-    with scope("along_z_1"):
-        along_z(1)
-    with scope("home_1"):
-        home(1)
+    hop_two(0, 1)
+    second_part(1, 0)
+    second_part(1, 1)
+    chip_sum(1, 0)
+    second_part(1, 2)
+    chip_sum(1, 1)
+    second_part(1, 3)
+    chip_sum(1, 2)
+    chip_sum(0, 3)
+    chip_sum(1, 3)
+    finish(0, 0)
+    hop_two(1, 0)
+    hop(1, 1, 2)
+    hop(1, 1, 3)
+    finish(0, 1)
+    hop_two(1, 1)
+    chunks = dims.feat // 256
+    weight_grads(0, chunks // 3)
+    finish(1, 0)
+    finish(1, 1)
+    weight_grads(chunks // 3, chunks)
+
+    @pl.when(jnp.logical_not(pair(z)))
+    def _():
+        uu[:, :, :, pl.ds(tile, tile)] = jnp.zeros((2, 4, grp, tile), BF)
 
     with scope("wait_home"):
-        for g in range(2):
-            zg = zh if g == 0 else zc
-            for d in range(4):
-                if g or d:
-                    got(back_ids[g, d], uu.at[zg, rows_of(up_y(4 - d) if d else y)])
-    slots = uu[...].reshape(2 * grp, 2 * tile)
+        wait_home()
+    total = uu[:, 0].astype(F32)
+    for d in range(1, 4):
+        total = total + uu[:, d].astype(F32)
+    slots = total.astype(BF).reshape(2 * grp, 2 * tile)
     same_token = (
         lax.broadcasted_iota(jnp.int32, (dims.tok, dims.tok), 0)
         == lax.broadcasted_iota(jnp.int32, (dims.tok, dims.tok), 1)
@@ -483,24 +547,12 @@
     with scope("last_swap"):
         for n, q in enumerate((x, (x + 3) % 4, (x + 1) % 4, (x + 2) % 4)):
             got(swap_last[n], outs.at[other, :, qcols(q)])
-    results = [
-        pltpu.make_async_copy(outs.at[n], d, ls.at[9 + n]) for n, d in enumerate((out_hbm, dx_hbm))
-    ]
-    for c in results:
-        c.start()
     with scope("drain"):
         for c in pending:
             c.wait_send()
         for g in range(2):
-            for d in range(1, 4):
-                zz = (z + d) % 4
-
-                @pl.when(pair(zz))
-                def _(g=g, d=d, zz=zz):
-                    copy(
-                        tile_ids[g, d, 1], yy.at[g, :, tcols(head(zz) + 1)], zr.at[g, d - 1, 1],
-                        sibling,
-                    ).wait_send()
+            for b in range(NY):
+                each_home(g, b, lambda c: c.wait_send())
 
         def sent(s):
             mine_ = cell(x, head(z) + s)
@@ -511,8 +563,15 @@
         for t in range(6):
             for i in (to_right, to_left, onward):
                 copy(i + t, cell(x, t), cell(x, t), sibling).wait_send()
-        for c in stores + results:
-            c.wait()
+
+
+def store_kernel(outs, gg, gu, gd, out, dx, gg_hbm, gu_hbm, gd_hbm, sems):
+    pairs = ((outs.at[0], out), (outs.at[1], dx), (gg, gg_hbm), (gu, gu_hbm), (gd, gd_hbm))
+    copies = [pltpu.make_async_copy(s, d, sems.at[n]) for n, (s, d) in enumerate(pairs)]
+    for c in copies:
+        c.start()
+    for c in copies:
+        c.wait()
 
 
 def on_device(tokens, cotangent, routes, router_weight, w_gate, w_up, w_down):
@@ -521,14 +580,18 @@
     half, quart, tile = dims.half, dims.quart, dims.tile
     vmem = pl.BlockSpec(memory_space=pltpu.VMEM)
     hbm = pl.BlockSpec(memory_space=pl.ANY)
-    wide = jax.ShapeDtypeStruct((2, grp, feat), BF)
-    narrow = jax.ShapeDtypeStruct((2, grp, hid), BF)
     whole = jax.ShapeDtypeStruct((dims.tok, feat), BF)
-    output, input_grad, slot_x, slot_dy, hidden, gate_dy, up_dy = pl.pallas_call(
+    tall, flat = (feat, hid), (hid, feat)
+    results = pl.pallas_call(
         functools.partial(experts_kernel, dims),
-        out_shape=(whole, whole, wide, wide, narrow, narrow, narrow),
+        out_shape=(
+            pltpu.VMEM((2, dims.tok, feat), BF),
+            pltpu.VMEM(tall, BF),
+            pltpu.VMEM(tall, BF),
+            pltpu.VMEM(flat, BF),
+        ),
         in_specs=[vmem] * 2 + [hbm] * 5,
-        out_specs=(hbm,) * 7,
+        out_specs=(vmem,) * 4,
         scratch_shapes=[
             pltpu.VMEM((dims.tok, feat), BF),
             pltpu.VMEM((2, grp, dims.tok), BF),
@@ -548,31 +611,29 @@
             pltpu.VMEM((2, grp, quart), BF),
             pltpu.VMEM((2, grp, quart), BF),
             pltpu.VMEM((2, grp, quart), BF),
-            pltpu.VMEM((2, 3, 2, grp, tile), BF),
-            pltpu.VMEM((2, grp, 2 * tile), BF),
-            pltpu.VMEM((2, grp, 2 * tile), BF),
-            pltpu.VMEM((2, dims.tok, feat), BF),
-            pltpu.SemaphoreType.DMA((128,)),
-            pltpu.SemaphoreType.DMA((128,)),
-            pltpu.SemaphoreType.DMA((11,)),
+            pltpu.VMEM((2, 4, grp, 2 * tile), BF),
+            pltpu.SemaphoreType.DMA((160,)),
+            pltpu.SemaphoreType.DMA((160,)),
+            pltpu.SemaphoreType.DMA((4,)),
         ],
         compiler_params=pltpu.CompilerParams(
-            collective_id=0, has_side_effects=True, vmem_limit_bytes=56 * 1024 * 1024
+            collective_id=0, has_side_effects=True, vmem_limit_bytes=48 * 1024 * 1024
         ),
         name="experts",
     )(routes.T, router_weight.T, tokens, cotangent, w_gate[0], w_up[0], w_down[0])
-    rows = 2 * grp
-    slot_x, slot_dy = slot_x.reshape(rows, feat), slot_dy.reshape(rows, feat)
-    hidden, gate_dy, up_dy = (a.reshape(rows, hid) for a in (hidden, gate_dy, up_dy))
-
-    def grad(left_rows, right_rows):
-        return lax.dot_general(
-            left_rows, right_rows, LEAD, preferred_element_type=F32
-        ).astype(BF)[None]
-
-    return (
-        output, input_grad, grad(slot_x, gate_dy), grad(slot_x, up_dy), grad(hidden, slot_dy)
-    )
+    output, input_grad, grad_gate, grad_up, grad_down = pl.pallas_call(
+        store_kernel,
+        out_shape=(
+            whole, whole, jax.ShapeDtypeStruct(tall, BF), jax.ShapeDtypeStruct(tall, BF),
+            jax.ShapeDtypeStruct(flat, BF),
+        ),
+        in_specs=[vmem] * 4,
+        out_specs=(hbm,) * 5,
+        scratch_shapes=[pltpu.SemaphoreType.DMA((5,))],
+        compiler_params=pltpu.CompilerParams(vmem_limit_bytes=16 * 1024 * 1024),
+        name="store",
+    )(*(pltpu.with_memory_space_constraint(r, pltpu.VMEM) for r in results))
+    return (output, input_grad, grad_gate[None], grad_up[None], grad_down[None])
 
 
 def solution(mesh):

time: 107 us -> 89 us (0.83)
  the two profiles are of different devices: /device:TPU:1 before, /device:TPU:31 now
where the time goes in v3:
time: 89 us; the launch traced here: 88.9 us
  Pallas kernels  88.3 us (99%)
    pallas_call x1, Pallas kernels, on_device(): pl.pallas_call(functools.partial(experts_kernel, dims), out_shape=(pltpu....  85.5 us
    pallas_call x1, Pallas kernels, on_device(): pl.pallas_call(store_kernel, out_shape=(whole, whole, jax.ShapeDtypeStruc...  2.74 us

profile of v3, /device:TPU:31, one launch (start us, length us, event | category | flops | bytes accessed | tf_op | source)
XLA Modules:
  0.0 88.9 jit_solution(7866342903009121274)
XLA Ops:
  0.6 85.5 %experts.1 = (bf16[2,128,3072]{2,1,0:T(8,128)(2,1)S(1)}, bf16[3072,256]{1,0:T(8,128)(2,1)S(1)}, bf16[3072,256]{1,0:T(8,128)(2,1)S(1)}, bf16[256,3072]{1,0:T(8,128)(2,1)S(1)}) custom-call(s32[2,128]{1,0:T(2,128)} %bitcast.11, f32[2,128]{1,0:T(2,128)} %bitcast.12, bf16[128,3072]{1,0:T(8,128)(2,1)} %tokens_hbm.1, bf16[128,3072]{1,0:T(8,128)(2,1)} %cotangent_hbm.1, ...), custom_call_target="tpu_custom_call" | custom-call | tf_op jit(solution)/shard_map/experts/pallas_call | solution.py:585
  86.2 2.7 %store.1 = (bf16[128,3072]{1,0:T(8,128)(2,1)}, bf16[128,3072]{1,0:T(8,128)(2,1)}, bf16[3072,256]{1,0:T(8,128)(2,1)}, bf16[3072,256]{1,0:T(8,128)(2,1)}, bf16[256,3072]{1,0:T(8,128)(2,1)}) custom-call(bf16[2,128,3072]{2,1,0:T(8,128)(2,1)S(1)} %get-tuple-element.14.outs, bf16[3072,256]{1,0:T(8,128)(2,1)S(1)} %get-tuple-element.15.gg, ...), custom_call_target="tpu_custom_call" | custom-call | tf_op jit(solution)/shard_map/store/pallas_call | solution.py:624

commit v4 on v3

--- a/solution.py
+++ b/solution.py
@@ -26,10 +26,10 @@
 
 def experts_kernel(
     dims,
-    routes, weights, tokens_hbm, cotangent_hbm, gate_hbm, up_hbm, down_hbm,
+    routes_hbm, weights_hbm, tokens_hbm, cotangent_hbm, gate_hbm, up_hbm, down_hbm,
     outs, gg, gu, gd,
-    mine, first, second, send,
-    arr, wg, wu, wd, hid, gdy, udy, tt, dd, rl1, rr1, rl2, rr2, yy, uu,
+    routes, weights, mine, first, second, send,
+    arr, wg, wu, wd, hid, gdy, udy, tt, dd, rl1, rr1, rl2, rr2, yy, zr, ww, uu,
     ss, rs, ls,
 ):
     scope = jax.named_scope
@@ -48,26 +48,32 @@
     right, left = dev(y, zh, z, (x + 1) % 4, k), dev(y, zh, z, (x + 3) % 4, k)
     sibling = dev(y, zh, z, x, other)
 
-    used = [0]
-    pending = []
+    used, out_used, drains = [0], [0], []
 
     def fresh():
         used[0] += 1
         return used[0] - 1
 
-    def copy(i, src, dst, to):
+    def group(region=None):
+        out_used[0] += 1
+        if region is not None:
+            drains.append((out_used[0] - 1, region))
+        return out_used[0] - 1
+
+    def copy(o, i, src, dst, to):
         return pltpu.make_async_remote_copy(
-            src_ref=src, dst_ref=dst, send_sem=ss.at[i], recv_sem=rs.at[i],
+            src_ref=src, dst_ref=dst, send_sem=ss.at[o], recv_sem=rs.at[i],
             device_id=to, device_id_type=MESH,
         )
 
-    def push(i, src, dst, to):
-        c = copy(i, src, dst, to)
-        c.start()
-        pending.append(c)
+    def push(o, i, src, dst, to):
+        copy(o, i, src, dst, to).start()
 
     def got(i, region):
-        copy(i, region, region, sibling).wait_recv()
+        copy(0, i, region, region, sibling).wait_recv()
+
+    def drained(o, region):
+        copy(o, 0, region, region, sibling).wait_send()
 
     def qcols(q, off=0, width=None):
         return pl.ds(pl.multiple_of(q * quart + off, 128), quart if width is None else width)
@@ -81,12 +87,19 @@
     barrier = pltpu.get_barrier_semaphore()
     partners = [right, left, sibling]
     for d in range(4):
+        partners.append(dev(up_y(d), 1 - zh, z, x, k))
         for turn in range(4):
             if d or turn:
                 partners.append(dev(up_y(d), zh, (z + turn) % 4, x, k))
-            partners.append(dev(up_y(d), 1 - zh, (z + turn) % 4, x, k))
     for p in partners:
         pl.semaphore_signal(barrier, inc=1, device_id=p, device_id_type=MESH)
+
+    tables = [
+        pltpu.make_async_copy(routes_hbm, routes, ls.at[4]),
+        pltpu.make_async_copy(weights_hbm, weights, ls.at[5]),
+    ]
+    for c in tables:
+        c.start()
 
     @pl.when(k == 0)
     def _():
@@ -102,6 +115,8 @@
     ]
     for c in loads:
         c.start()
+    for c in tables:
+        c.wait()
 
     experts = NY * NZH
     seat = lax.broadcasted_iota(jnp.int32, (experts, dims.tok), 0)
@@ -137,33 +152,46 @@
     with scope("barrier"):
         pl.semaphore_wait(barrier, len(partners))
     ring_order = [(0, 2), (1, 0), (1, 1), (1, 3), (1, 2)]
-    send_ids = {(g, d): fresh() for g in range(2) for d in range(4)}
-    both_ids = {(g, d): fresh() for g in range(2) for d in range(4)}
+    send_ids = {b: fresh() for b in ring_order + [(0, 1), (0, 3)]}
+    both_ids = [fresh() for _ in range(2)]
     ring = {b: [fresh() for _ in range(4)] for b in ring_order}
+    rows5 = pl.ds(0, len(ring_order) * cap // 3)
+    fives = arr.at[0, 0, rows5, pl.ds(0, 3 * quart)]
+    fives_half = arr.at[0, 0, rows5, pl.ds(0, 3 * half)]
+    pair_ids = {d: fresh() for d in range(4)}
+    own_half, pair_half = (z % 2) * half, (1 - z % 2) * half
+    partner = dev(y, zh, z + 1 - 2 * (z % 2), x, k)
+    out_quart = group(send.at[0, pl.ds(0, cap), pl.ds(0, 3 * quart)])
+    out_pair = group(arr.at[0, 0, pl.ds(0, cap), pl.ds(0, 2 * quart)])
+    out_full = group(send.at[0, pl.ds(0, 2 * cap)])
+    out_both = [group(arr.at[0, 0]) for _ in range(2)]
+    out_ring = [group(r) for r in (fives, fives, fives_half, fives_half)]
     for d in (0, 1, 3, 2):
         push(
-            send_ids[1, d],
-            send.at[zc, rows_of(up_y(d)), qcols(x)],
-            arr.at[k, zh, rows_of(y), qcols(x)],
+            out_quart, send_ids[1, d],
+            send.at[zc, rows_of(up_y(d)), qcols(x, own_half, half)],
+            arr.at[k, zh, rows_of(y), qcols(x, own_half, half)],
             dev(up_y(d), zc, z, x, k),
         )
     with scope("fill_same"):
         for q in (x, (x + 1) % 4, (x + 2) % 4, (x + 3) % 4):
             fill(zh, qcols(q))
     push(
-        send_ids[0, 2],
+        out_quart, send_ids[0, 2],
         send.at[zh, rows_of(up_y(2)), qcols(x)],
         arr.at[k, zh, rows_of(y), qcols(x)],
         dev(up_y(2), zh, z, x, k),
     )
     for d in (1, 3):
         push(
-            send_ids[0, d],
+            out_full, send_ids[0, d],
             send.at[zh, rows_of(up_y(d))],
             arr.at[k, zh, rows_of(y)],
             dev(up_y(d), zh, z, x, k),
         )
-    push(both_ids[0, 0], send.at[zh, rows_of(y)], arr.at[k, zh, rows_of(y)], sibling)
+    push(
+        out_both[0], both_ids[0], send.at[zh, rows_of(y)], arr.at[k, zh, rows_of(y)], sibling
+    )
     arr[k, zh, rows_of(y)] = send[zh, rows_of(y)]
 
     def block_of(b, *cols):
@@ -171,38 +199,45 @@
         rows = rows_of(up_y(4 - d) if d else y)
         return arr.at[(k, zc if g else zh, rows) + cols]
 
+    def crossed(d):
+        with scope(f"crossed_{d}"):
+            part_ = block_of((1, d), qcols(x, own_half, half))
+            got(send_ids[1, d], part_)
+            push(out_pair, pair_ids[d], part_, part_, partner)
+
     def ring_one(b):
         with scope(f"ring_one_{b[0]}{b[1]}"):
             near = block_of(b, qcols(x))
-            got(send_ids[b], near)
-            push(ring[b][0], near, near, right)
-            push(ring[b][1], near, near, left)
+            if b[0]:
+                got(pair_ids[b[1]], block_of(b, qcols(x, pair_half, half)))
+            else:
+                got(send_ids[b], near)
+            push(out_ring[0], ring[b][0], near, near, right)
+            push(out_ring[1], ring[b][1], near, near, left)
 
     def ring_two(b):
         with scope(f"ring_two_{b[0]}{b[1]}"):
             got(ring[b][0], block_of(b, qcols((x + 3) % 4)))
             near = block_of(b, qcols((x + 3) % 4, 0, half))
-            push(ring[b][2], near, near, right)
+            push(out_ring[2], ring[b][2], near, near, right)
             got(ring[b][1], block_of(b, qcols((x + 1) % 4)))
             near = block_of(b, qcols((x + 1) % 4, half, half))
-            push(ring[b][3], near, near, left)
+            push(out_ring[3], ring[b][3], near, near, left)
 
     def ring_end(b):
         with scope(f"ring_end_{b[0]}{b[1]}"):
             got(ring[b][2], block_of(b, qcols((x + 2) % 4, 0, half)))
             got(ring[b][3], block_of(b, qcols((x + 2) % 4, half, half)))
-            push(both_ids[b], block_of(b), block_of(b), sibling)
+            push(out_both[b[0]], both_ids[b[0]], block_of(b), block_of(b), sibling)
 
     def same_block(d):
         with scope(f"same_block_{d}"):
             got(send_ids[0, d], block_of((0, d)))
-            push(both_ids[0, d], block_of((0, d)), block_of((0, d)), sibling)
+            push(out_both[0], both_ids[0], block_of((0, d)), block_of((0, d)), sibling)
 
     def both_here(g):
         with scope(f"both_here_{g}"):
-            for d in range(4):
-                rows = rows_of(up_y(4 - d) if d else y)
-                got(both_ids[g, d], arr.at[other, zc if g else zh, rows])
+            got(both_ids[g], arr.at[other, zc if g else zh])
 
     def first_stage(g):
         zg = zh if g == 0 else zc
@@ -217,6 +252,10 @@
 
     quarters = [(x + 2) % 4, (x + 1) % 4, (x + 3) % 4, x]
     swap_ids = {(g, n): fresh() for g in range(2) for n in range(4)}
+    out_swap = [group(dd.at[g]) for g in range(2)]
+    out_hop = {
+        (g, n): group(tt.at[g, 0, :, pl.ds(0, 3 * half)]) for g in range(2) for n in range(2)
+    }
 
     hop_ids = {(g, h, n): fresh() for g in range(2) for h in range(2) for n in range(6)}
     part = grp // 2
@@ -236,7 +275,7 @@
             target = (rl1, rr1)[n].at[g, rows]
         else:
             target = (rl2 if n % 2 == 0 else rr2).at[g, rows, pl.ds(off, half)]
-        push(hop_ids[g, h, n], source, target, right if n % 2 == 0 else left)
+        push(out_hop[g, n % 2], hop_ids[g, h, n], source, target, right if n % 2 == 0 else left)
 
     def chip_sum(g, n):
         with scope(f"chip_sum_{g}{n}"):
@@ -268,7 +307,10 @@
 
         with scope(f"second_{g}{n}"):
             lax.fori_loop(0, 3, body, 0)
-        push(swap_ids[g, n], tt.at[g, other, :, qcols(q)], dd.at[g, :, qcols(q)], sibling)
+        push(
+            out_swap[g], swap_ids[g, n], tt.at[g, other, :, qcols(q)], dd.at[g, :, qcols(q)],
+            sibling,
+        )
 
     def hop_two(g, h):
         with scope(f"hop_two_{g}{h}"):
@@ -288,31 +330,69 @@
     def pair(zz):
         return (zz + k) % 2 == 0
 
-    home_ids = {(g, d): [fresh() for _ in range(NY)][0] for g in range(2) for d in range(4)}
-
-    def home_copy(g, d, b, wide):
+    home_ids = [fresh() for _ in range(5)]
+    along_ids = {(h, d): fresh() for h in range(2) for d in range(1, 4)}
+    out_home = [group() for _ in range(5)]
+    out_along = {d: group() for d in range(1, 4)}
+
+    def home_copy(d, b, wide):
         width = 2 * tile if wide else tile
         zz = (z + d) % 4
         return pltpu.make_async_remote_copy(
-            src_ref=yy.at[g, rows_of(b), pl.ds(pl.multiple_of(head(zz) * tile, 128), width)],
+            src_ref=yy.at[0, rows_of(b), pl.ds(pl.multiple_of(head(zz) * tile, 128), width)],
             dst_ref=uu.at[zh, d, rows_of(y), pl.ds(0, width)],
-            send_sem=ss.at[home_ids[g, d] + b], recv_sem=rs.at[home_ids[g, d] + y],
-            device_id=dev(b, zh if g == 0 else zc, zz, x, k), device_id_type=MESH,
+            send_sem=ss.at[out_home[d]], recv_sem=rs.at[home_ids[d]],
+            device_id=dev(b, zh, zz, x, k), device_id_type=MESH,
         )
 
     def by_width(zz, action):
         pl.when(pair(zz))(lambda: action(True))
         pl.when(jnp.logical_not(pair(zz)))(lambda: action(False))
 
-    def each_home(g, b, action):
-        for d in (1, 3, 2, 0):
+    def each_home(b):
+        for d in (2, 1, 3, 0):
             zz = (z + d) % 4
-            if g == 0 and d == 0:
+            if d == 0:
                 pl.when(b != y)(
-                    lambda d=d, zz=zz: by_width(zz, lambda wide: action(home_copy(g, d, b, wide)))
+                    lambda d=d, zz=zz: by_width(zz, lambda wide: home_copy(d, b, wide).start())
                 )
             else:
-                by_width(zz, lambda wide, d=d: action(home_copy(g, d, b, wide)))
+                by_width(zz, lambda wide, d=d: home_copy(d, b, wide).start())
+
+    def along(h):
+        rows = rows_h(h)
+        for d in (2, 1, 3):
+            zz = (z + d) % 4
+
+            def go(wide, d=d, zz=zz):
+                width = 2 * tile if wide else tile
+                push(
+                    out_along[d], along_ids[h, d],
+                    yy.at[1, rows, pl.ds(pl.multiple_of(head(zz) * tile, 128), width)],
+                    zr.at[d - 1, rows, pl.ds(0, width)], dev(y, zh, zz, x, k),
+                )
+
+            by_width(zz, go)
+
+    def collect(h):
+        def add(wide):
+            rows, width = rows_h(h), 2 * tile if wide else tile
+            for d in range(1, 4):
+                got(along_ids[h, d], zr.at[d - 1, rows, pl.ds(0, width)])
+            for s in range(2 if wide else 1):
+                at = pl.ds(s * tile, tile)
+                total = yy[1, rows, tcols(head(z) + s)].astype(F32)
+                for d in range(1, 4):
+                    total = total + zr[d - 1, rows, at].astype(F32)
+                ww[rows, at] = total.astype(BF)
+            for b in (2 * h, 2 * h + 1):
+                push(
+                    out_home[4], home_ids[4], ww.at[rows_of(b), pl.ds(0, width)],
+                    uu.at[zh, 0, rows_of(y), pl.ds(0, width)], dev(b, zc, z, x, k),
+                )
+
+        with scope(f"collect_{h}"):
+            by_width(z, add)
 
     def finish(g, h):
         with scope(f"finish_{g}{h}"):
@@ -329,36 +409,29 @@
                 + rl2[g, rows].astype(F32)
                 + rr2[g, rows].astype(F32)
             ).astype(BF)
+            if g == 1:
+                along(h)
+                return
             for b in (2 * h, 2 * h + 1):
-                each_home(g, b, lambda c: c.start())
-                if g == 0:
-
-                    @pl.when(b == y)
-                    def _(b=b):
-                        def keep(wide):
-                            for s in range(2 if wide else 1):
-                                uu[zh, 0, rows_of(y), pl.ds(s * tile, tile)] = yy[
-                                    0, rows_of(b), tcols(head(z) + s)
-                                ]
-
-                        by_width(z, keep)
+                each_home(b)
+
+                @pl.when(b == y)
+                def _(b=b):
+                    def keep(wide):
+                        for s in range(2 if wide else 1):
+                            uu[zh, 0, rows_of(y), pl.ds(s * tile, tile)] = yy[
+                                0, rows_of(b), tcols(head(z) + s)
+                            ]
+
+                    by_width(z, keep)
 
     def wait_home():
         def arrived(wide):
             width = 2 * tile if wide else tile
-            for g in range(2):
-                for d in range(4):
-                    for b in range(NY):
-                        region = uu.at[zc if g else zh, d, rows_of(b), pl.ds(0, width)]
-                        wait = pltpu.make_async_remote_copy(
-                            src_ref=region, dst_ref=region, send_sem=ss.at[home_ids[g, d] + b],
-                            recv_sem=rs.at[home_ids[g, d] + b], device_id=sibling,
-                            device_id_type=MESH,
-                        )
-                        if g == 0 and d == 0:
-                            pl.when(b != y)(wait.wait_recv)
-                        else:
-                            wait.wait_recv()
+            for d in range(4):
+                rows = grp if d else (NY - 1) * cap
+                got(home_ids[d], uu.at[zh, d, pl.ds(0, rows), pl.ds(0, width)])
+            got(home_ids[4], uu.at[zc, 0, :, pl.ds(0, width)])
 
         by_width(z, arrived)
 
@@ -385,15 +458,19 @@
             lax.fori_loop(begin, end, body, 0)
 
     ring_one((0, 2))
+    crossed(0)
+    crossed(1)
+    ring_two((0, 2))
+    crossed(3)
     ring_one((1, 0))
-    ring_two((0, 2))
+    crossed(2)
     ring_one((1, 1))
     ring_end((0, 2))
+    ring_two((1, 0))
+    ring_one((1, 3))
+    ring_one((1, 2))
     same_block(1)
     same_block(3)
-    ring_one((1, 3))
-    ring_two((1, 0))
-    ring_one((1, 2))
     ring_two((1, 1))
     with scope("weights_here"):
         for c in loads:
@@ -401,8 +478,8 @@
     both_here(0)
     with scope("first_0"):
         first_stage(0)
+    ring_two((1, 3))
     ring_end((1, 0))
-    ring_two((1, 3))
     second_part(0, 0)
     ring_two((1, 2))
     ring_end((1, 1))
@@ -414,32 +491,34 @@
     second_part(0, 3)
     chip_sum(0, 2)
     ring_end((1, 2))
+    chip_sum(0, 3)
     hop_two(0, 0)
     hop(0, 1, 2)
     hop(0, 1, 3)
     both_here(1)
     with scope("first_1"):
         first_stage(1)
+    second_part(1, 0)
     hop_two(0, 1)
-    second_part(1, 0)
     second_part(1, 1)
     chip_sum(1, 0)
     second_part(1, 2)
     chip_sum(1, 1)
     second_part(1, 3)
     chip_sum(1, 2)
-    chip_sum(0, 3)
-    chip_sum(1, 3)
     finish(0, 0)
     hop_two(1, 0)
     hop(1, 1, 2)
     hop(1, 1, 3)
+    chip_sum(1, 3)
     finish(0, 1)
     hop_two(1, 1)
     chunks = dims.feat // 256
     weight_grads(0, chunks // 3)
     finish(1, 0)
     finish(1, 1)
+    collect(0)
+    collect(1)
     weight_grads(chunks // 3, chunks)
 
     @pl.when(jnp.logical_not(pair(z)))
@@ -448,10 +527,11 @@
 
     with scope("wait_home"):
         wait_home()
-    total = uu[:, 0].astype(F32)
+    total = uu[zh, 0].astype(F32)
     for d in range(1, 4):
-        total = total + uu[:, d].astype(F32)
-    slots = total.astype(BF).reshape(2 * grp, 2 * tile)
+        total = total + uu[zh, d].astype(F32)
+    uu[zh, 0] = total.astype(BF)
+    slots = uu[:, 0].reshape(2 * grp, 2 * tile)
     same_token = (
         lax.broadcasted_iota(jnp.int32, (dims.tok, dims.tok), 0)
         == lax.broadcasted_iota(jnp.int32, (dims.tok, dims.tok), 1)
@@ -484,8 +564,11 @@
     last_ids = {(d, s): fresh() for d in range(1, 4) for s in range(2)}
     to_right = [fresh() for _ in range(6)][0]
     to_left = [fresh() for _ in range(6)][0]
-    onward = [fresh() for _ in range(6)][0]
-    swap_last = [fresh() for _ in range(4)]
+    onward, swap_last = fresh(), fresh()
+    out_last = [group(), group()]
+    one_quart = outs.at[0, :, pl.ds(0, quart)]
+    out_right, out_left, out_onward = (group(one_quart) for _ in range(3))
+    out_swap_last = group(outs.at[0])
 
     def cell(q, t):
         return outs.at[k, :, tcols(t, q * quart)]
@@ -495,15 +578,15 @@
         pl.when(pair(zz))(lambda: action(1))
 
     def near_x(t):
-        copy(to_right + t, cell(x, t), cell(x, t), right).start()
-        copy(to_left + t, cell(x, t), cell(x, t), left).start()
+        push(out_right, to_right + t, cell(x, t), cell(x, t), right)
+        push(out_left, to_left + t, cell(x, t), cell(x, t), left)
 
     def first_out(s):
         t = head(z) + s
         near_x(t)
         for d in (1, 3, 2):
             to = dev(y, zh, (z + d) % 4, x, k)
-            copy(last_ids[d, s], cell(x, t), cell(x, t), to).start()
+            push(out_last[s], last_ids[d, s], cell(x, t), cell(x, t), to)
 
     each_tile(z, first_out)
     with scope("last_z"):
@@ -516,7 +599,11 @@
                 near_x(t)
 
             each_tile(zz, relay)
-    push(swap_last[0], outs.at[k, :, qcols(x)], outs.at[k, :, qcols(x)], sibling)
+    def swap_quarter(q):
+        cells = outs.at[k, :, qcols(q)]
+        push(out_swap_last, swap_last, cells, cells, sibling)
+
+    swap_quarter(x)
     with scope("last_x"):
         for d in (0, 1, 3, 2):
             zz = (z + 4 - d) % 4
@@ -528,41 +615,39 @@
 
                 @pl.when(t < 3)
                 def _():
-                    copy(onward + t, from_left, from_left, right).start()
+                    push(out_onward, onward, from_left, from_left, right)
 
                 got(to_left + t, from_right)
 
                 @pl.when(t >= 3)
                 def _():
-                    copy(onward + t, from_right, from_right, left).start()
+                    push(out_onward, onward, from_right, from_right, left)
 
             each_tile(zz, onwards)
-    for n, q in ((1, (x + 3) % 4), (2, (x + 1) % 4)):
-        push(swap_last[n], outs.at[k, :, qcols(q)], outs.at[k, :, qcols(q)], sibling)
+    swap_quarter((x + 3) % 4)
+    swap_quarter((x + 1) % 4)
     with scope("last_far"):
-        for t in range(6):
-            got(onward + t, cell((x + 2) % 4, t))
-    far = outs.at[k, :, qcols((x + 2) % 4)]
-    push(swap_last[3], far, far, sibling)
+        got(onward, outs.at[k, :, qcols((x + 2) % 4)])
+    swap_quarter((x + 2) % 4)
     with scope("last_swap"):
-        for n, q in enumerate((x, (x + 3) % 4, (x + 1) % 4, (x + 2) % 4)):
-            got(swap_last[n], outs.at[other, :, qcols(q)])
+        got(swap_last, outs.at[other])
     with scope("drain"):
-        for c in pending:
-            c.wait_send()
-        for g in range(2):
-            for b in range(NY):
-                each_home(g, b, lambda c: c.wait_send())
-
-        def sent(s):
-            mine_ = cell(x, head(z) + s)
-            for d in range(1, 4):
-                copy(last_ids[d, s], mine_, mine_, sibling).wait_send()
-
-        each_tile(z, sent)
-        for t in range(6):
-            for i in (to_right, to_left, onward):
-                copy(i + t, cell(x, t), cell(x, t), sibling).wait_send()
+        for o, region in drains:
+            drained(o, region)
+        for d in range(4):
+            rows = grp if d else (NY - 1) * cap
+
+            def sent_home(wide, d=d, rows=rows):
+                width = 2 * tile if wide else tile
+                drained(out_home[d], yy.at[0, pl.ds(0, rows), pl.ds(0, width)])
+                if d:
+                    drained(out_along[d], yy.at[1, :, pl.ds(0, width)])
+                else:
+                    drained(out_home[4], ww.at[:, pl.ds(0, width)])
+
+            by_width((z + d) % 4, sent_home)
+        each_tile(z, lambda s: drained(out_last[s], outs.at[0, :, pl.ds(0, 3 * tile)]))
+    assert used[0] == rs.shape[0] and out_used[0] == ss.shape[0], (used, out_used)
 
 
 def store_kernel(outs, gg, gu, gd, out, dx, gg_hbm, gu_hbm, gd_hbm, sems):
@@ -590,9 +675,11 @@
             pltpu.VMEM(tall, BF),
             pltpu.VMEM(flat, BF),
         ),
-        in_specs=[vmem] * 2 + [hbm] * 5,
+        in_specs=[hbm] * 7,
         out_specs=(vmem,) * 4,
         scratch_shapes=[
+            pltpu.VMEM(routes.T.shape, jnp.int32),
+            pltpu.VMEM(routes.T.shape, F32),
             pltpu.VMEM((dims.tok, feat), BF),
             pltpu.VMEM((2, grp, dims.tok), BF),
             pltpu.VMEM((2, grp, dims.tok), BF),
@@ -611,10 +698,12 @@
             pltpu.VMEM((2, grp, quart), BF),
             pltpu.VMEM((2, grp, quart), BF),
             pltpu.VMEM((2, grp, quart), BF),
+            pltpu.VMEM((3, grp, 2 * tile), BF),
+            pltpu.VMEM((grp, 2 * tile), BF),
             pltpu.VMEM((2, 4, grp, 2 * tile), BF),
-            pltpu.SemaphoreType.DMA((160,)),
-            pltpu.SemaphoreType.DMA((160,)),
-            pltpu.SemaphoreType.DMA((4,)),
+            pltpu.SemaphoreType.DMA((29,)),
+            pltpu.SemaphoreType.DMA((96,)),
+            pltpu.SemaphoreType.DMA((6,)),
         ],
         compiler_params=pltpu.CompilerParams(
             collective_id=0, has_side_effects=True, vmem_limit_bytes=48 * 1024 * 1024

time: 89 us -> 83.7 us (0.940)
  the two profiles are of different devices: /device:TPU:31 before, /device:TPU:1 now
where the time goes in v4:
time: 83.7 us; the launch traced here: 83.6 us
  Pallas kernels  83 us (99%)
    pallas_call x1, Pallas kernels, on_device(): pl.pallas_call(functools.partial(experts_kernel, dims), out_shape=(pltpu....  80.2 us
    pallas_call x1, Pallas kernels, on_device(): pl.pallas_call(store_kernel, out_shape=(whole, whole, jax.ShapeDtypeStruc...  2.74 us

profile of v4, /device:TPU:1, one launch (start us, length us, event | category | flops | bytes accessed | tf_op | source)
XLA Modules:
  0.0 83.6 jit_solution(11282416715164669099)
XLA Ops:
  0.6 80.2 %experts.1 = (bf16[2,128,3072]{2,1,0:T(8,128)(2,1)S(1)}, bf16[3072,256]{1,0:T(8,128)(2,1)S(1)}, bf16[3072,256]{1,0:T(8,128)(2,1)S(1)}, bf16[256,3072]{1,0:T(8,128)(2,1)S(1)}) custom-call(s32[2,128]{1,0:T(2,128)} %bitcast.11, f32[2,128]{1,0:T(2,128)} %bitcast.12, bf16[128,3072]{1,0:T(8,128)(2,1)} %tokens_hbm.1, bf16[128,3072]{1,0:T(8,128)(2,1)} %cotangent_hbm.1, ...), custom_call_target="tpu_custom_call" | custom-call | tf_op jit(solution)/shard_map/experts/pallas_call | solution.py:670
  80.9 2.7 %store.1 = (bf16[128,3072]{1,0:T(8,128)(2,1)}, bf16[128,3072]{1,0:T(8,128)(2,1)}, bf16[3072,256]{1,0:T(8,128)(2,1)}, bf16[3072,256]{1,0:T(8,128)(2,1)}, bf16[256,3072]{1,0:T(8,128)(2,1)}) custom-call(bf16[2,128,3072]{2,1,0:T(8,128)(2,1)S(1)} %get-tuple-element.14.outs, bf16[3072,256]{1,0:T(8,128)(2,1)S(1)} %get-tuple-element.15.gg, ...), custom_call_target="tpu_custom_call" | custom-call | tf_op jit(solution)/shard_map/store/pallas_call | solution.py:713

commit v5 on v4

--- a/solution.py
+++ b/solution.py
@@ -154,7 +154,7 @@
     ring_order = [(0, 2), (1, 0), (1, 1), (1, 3), (1, 2)]
     send_ids = {b: fresh() for b in ring_order + [(0, 1), (0, 3)]}
     both_ids = [fresh() for _ in range(2)]
-    ring = {b: [fresh() for _ in range(4)] for b in ring_order}
+    ring = {b: [fresh() for _ in range(3)] for b in ring_order}
     rows5 = pl.ds(0, len(ring_order) * cap // 3)
     fives = arr.at[0, 0, rows5, pl.ds(0, 3 * quart)]
     fives_half = arr.at[0, 0, rows5, pl.ds(0, 3 * half)]
@@ -222,12 +222,11 @@
             push(out_ring[2], ring[b][2], near, near, right)
             got(ring[b][1], block_of(b, qcols((x + 1) % 4)))
             near = block_of(b, qcols((x + 1) % 4, half, half))
-            push(out_ring[3], ring[b][3], near, near, left)
+            push(out_ring[3], ring[b][2], near, near, left)
 
     def ring_end(b):
         with scope(f"ring_end_{b[0]}{b[1]}"):
-            got(ring[b][2], block_of(b, qcols((x + 2) % 4, 0, half)))
-            got(ring[b][3], block_of(b, qcols((x + 2) % 4, half, half)))
+            got(ring[b][2], block_of(b, qcols((x + 2) % 4)))
             push(out_both[b[0]], both_ids[b[0]], block_of(b), block_of(b), sibling)
 
     def same_block(d):
@@ -257,25 +256,25 @@
         (g, n): group(tt.at[g, 0, :, pl.ds(0, 3 * half)]) for g in range(2) for n in range(2)
     }
 
-    hop_ids = {(g, h, n): fresh() for g in range(2) for h in range(2) for n in range(6)}
-    part = grp // 2
+    parts = (2, 4)
+    hop_ids = {(g, h, n): fresh() for g in range(2) for h in range(parts[g]) for n in range(4)}
 
     def plus(a, b):
         return (a.astype(F32) + b.astype(F32)).astype(BF)
 
-    def rows_h(h):
-        return pl.ds(h * part, part)
+    def rows_h(g, h):
+        return pl.ds(h * (grp // parts[g]), grp // parts[g])
 
     def hop(g, h, n):
         q = quarters[(0, 0, 1, 2, 1, 2)[n]]
         off = (0, half, half, 0, 0, half)[n]
-        rows = rows_h(h)
+        rows = rows_h(g, h)
         source = tt.at[g, k, rows, qcols(q, off, half)]
         if n < 2:
             target = (rl1, rr1)[n].at[g, rows]
         else:
             target = (rl2 if n % 2 == 0 else rr2).at[g, rows, pl.ds(off, half)]
-        push(out_hop[g, n % 2], hop_ids[g, h, n], source, target, right if n % 2 == 0 else left)
+        push(out_hop[g, n % 2], hop_ids[g, h, n - 2 if n > 3 else n], source, target, right if n % 2 == 0 else left)
 
     def chip_sum(g, n):
         with scope(f"chip_sum_{g}{n}"):
@@ -283,7 +282,7 @@
             got(swap_ids[g, n], dd.at[g, :, qcols(q)])
             tt[g, k, :, qcols(q)] = plus(tt[g, k, :, qcols(q)], dd[g, :, qcols(q)])
             if n == 0:
-                for h in range(2):
+                for h in range(parts[g]):
                     hop(g, h, 0)
                     hop(g, h, 1)
             if n in (1, 2):
@@ -306,7 +305,8 @@
             return carry
 
         with scope(f"second_{g}{n}"):
-            lax.fori_loop(0, 3, body, 0)
+            for c in range(3):
+                body(c, 0)
         push(
             out_swap[g], swap_ids[g, n], tt.at[g, other, :, qcols(q)], dd.at[g, :, qcols(q)],
             sibling,
@@ -314,7 +314,7 @@
 
     def hop_two(g, h):
         with scope(f"hop_two_{g}{h}"):
-            rows = rows_h(h)
+            rows = rows_h(g, h)
             got(hop_ids[g, h, 0], rl1.at[g, rows])
             at = qcols(quarters[1], 0, half)
             tt[g, k, rows, at] = plus(tt[g, k, rows, at], rl1[g, rows])
@@ -331,7 +331,7 @@
         return (zz + k) % 2 == 0
 
     home_ids = [fresh() for _ in range(5)]
-    along_ids = {(h, d): fresh() for h in range(2) for d in range(1, 4)}
+    along_ids = {(h, d): fresh() for h in range(parts[1]) for d in range(1, 4)}
     out_home = [group() for _ in range(5)]
     out_along = {d: group() for d in range(1, 4)}
 
@@ -360,7 +360,7 @@
                 by_width(zz, lambda wide, d=d: home_copy(d, b, wide).start())
 
     def along(h):
-        rows = rows_h(h)
+        rows = rows_h(1, h)
         for d in (2, 1, 3):
             zz = (z + d) % 4
 
@@ -376,7 +376,7 @@
 
     def collect(h):
         def add(wide):
-            rows, width = rows_h(h), 2 * tile if wide else tile
+            rows, width = rows_h(1, h), 2 * tile if wide else tile
             for d in range(1, 4):
                 got(along_ids[h, d], zr.at[d - 1, rows, pl.ds(0, width)])
             for s in range(2 if wide else 1):
@@ -385,25 +385,19 @@
                 for d in range(1, 4):
                     total = total + zr[d - 1, rows, at].astype(F32)
                 ww[rows, at] = total.astype(BF)
-            for b in (2 * h, 2 * h + 1):
-                push(
-                    out_home[4], home_ids[4], ww.at[rows_of(b), pl.ds(0, width)],
-                    uu.at[zh, 0, rows_of(y), pl.ds(0, width)], dev(b, zc, z, x, k),
-                )
+            push(
+                out_home[4], home_ids[4], ww.at[rows, pl.ds(0, width)],
+                uu.at[zh, 0, rows_of(y), pl.ds(0, width)], dev(h, zc, z, x, k),
+            )
 
         with scope(f"collect_{h}"):
             by_width(z, add)
 
     def finish(g, h):
         with scope(f"finish_{g}{h}"):
-            rows = rows_h(h)
-            for n in (2, 3, 4, 5):
-                got(
-                    hop_ids[g, h, n],
-                    (rl2 if n % 2 == 0 else rr2).at[
-                        g, rows, pl.ds((0, half, half, 0, 0, half)[n], half)
-                    ],
-                )
+            rows = rows_h(g, h)
+            got(hop_ids[g, h, 2], rl2.at[g, rows])
+            got(hop_ids[g, h, 3], rr2.at[g, rows])
             yy[g, rows] = (
                 tt[g, k, rows, qcols(x)].astype(F32)
                 + rl2[g, rows].astype(F32)
@@ -478,17 +472,17 @@
     both_here(0)
     with scope("first_0"):
         first_stage(0)
+    second_part(0, 0)
     ring_two((1, 3))
     ring_end((1, 0))
-    second_part(0, 0)
     ring_two((1, 2))
+    second_part(0, 1)
     ring_end((1, 1))
-    second_part(0, 1)
     chip_sum(0, 0)
-    ring_end((1, 3))
     second_part(0, 2)
     chip_sum(0, 1)
     second_part(0, 3)
+    ring_end((1, 3))
     chip_sum(0, 2)
     ring_end((1, 2))
     chip_sum(0, 3)
@@ -507,19 +501,32 @@
     second_part(1, 3)
     chip_sum(1, 2)
     finish(0, 0)
+    chunks = dims.feat // 256
+    weight_grads(0, chunks // 3)
     hop_two(1, 0)
     hop(1, 1, 2)
     hop(1, 1, 3)
-    chip_sum(1, 3)
     finish(0, 1)
     hop_two(1, 1)
-    chunks = dims.feat // 256
-    weight_grads(0, chunks // 3)
+    hop(1, 2, 2)
+    hop(1, 2, 3)
+    chip_sum(1, 3)
+    hop_two(1, 2)
+    hop(1, 3, 2)
+    hop(1, 3, 3)
+    hop_two(1, 3)
     finish(1, 0)
+    weight_grads(chunks // 3, chunks // 2)
     finish(1, 1)
+    weight_grads(chunks // 2, 2 * chunks // 3)
+    finish(1, 2)
     collect(0)
+    finish(1, 3)
     collect(1)
-    weight_grads(chunks // 3, chunks)
+    weight_grads(2 * chunks // 3, 5 * chunks // 6)
+    collect(2)
+    collect(3)
+    weight_grads(5 * chunks // 6, chunks)
 
     @pl.when(jnp.logical_not(pair(z)))
     def _():
@@ -702,7 +709,7 @@
             pltpu.VMEM((grp, 2 * tile), BF),
             pltpu.VMEM((2, 4, grp, 2 * tile), BF),
             pltpu.SemaphoreType.DMA((29,)),
-            pltpu.SemaphoreType.DMA((96,)),
+            pltpu.SemaphoreType.DMA((97,)),
             pltpu.SemaphoreType.DMA((6,)),
         ],
         compiler_params=pltpu.CompilerParams(

time: 83.7 us -> 80.6 us (0.963); the launches traced: 83.6 us -> 79.4 us
  Pallas kernels: 83 us -> 78.7 us
    pallas_call x1, Pallas kernels: 80.2 us -> 76 us  [on_device(): pl.pallas_call(functools.partial(experts_kernel, dims), out_shape=(pltpu....]
where the time goes in v5:
time: 80.6 us; the launch traced here: 79.4 us
  Pallas kernels  78.7 us (98%)
    pallas_call x1, Pallas kernels, on_device(): pl.pallas_call(functools.partial(experts_kernel, dims), out_shape=(pltpu....  76 us
    pallas_call x1, Pallas kernels, on_device(): pl.pallas_call(store_kernel, out_shape=(whole, whole, jax.ShapeDtypeStruc...  2.74 us

profile of v5, /device:TPU:1, one launch (start us, length us, event | category | flops | bytes accessed | tf_op | source)
XLA Modules:
  0.0 79.4 jit_solution(5956797886185306093)
XLA Ops:
  0.6 76.0 %experts.1 = (bf16[2,128,3072]{2,1,0:T(8,128)(2,1)S(1)}, bf16[3072,256]{1,0:T(8,128)(2,1)S(1)}, bf16[3072,256]{1,0:T(8,128)(2,1)S(1)}, bf16[256,3072]{1,0:T(8,128)(2,1)S(1)}) custom-call(s32[2,128]{1,0:T(2,128)} %bitcast.11, f32[2,128]{1,0:T(2,128)} %bitcast.12, bf16[128,3072]{1,0:T(8,128)(2,1)} %tokens_hbm.1, bf16[128,3072]{1,0:T(8,128)(2,1)} %cotangent_hbm.1, ...), custom_call_target="tpu_custom_call" | custom-call | tf_op jit(solution)/shard_map/experts/pallas_call | solution.py:677
  76.6 2.7 %store.1 = (bf16[128,3072]{1,0:T(8,128)(2,1)}, bf16[128,3072]{1,0:T(8,128)(2,1)}, bf16[3072,256]{1,0:T(8,128)(2,1)}, bf16[3072,256]{1,0:T(8,128)(2,1)}, bf16[256,3072]{1,0:T(8,128)(2,1)}) custom-call(bf16[2,128,3072]{2,1,0:T(8,128)(2,1)S(1)} %get-tuple-element.14.outs, bf16[3072,256]{1,0:T(8,128)(2,1)S(1)} %get-tuple-element.15.gg, ...), custom_call_target="tpu_custom_call" | custom-call | tf_op jit(solution)/shard_map/store/pallas_call | solution.py:720

commit v6 on v5

--- a/solution.py
+++ b/solution.py
@@ -29,7 +29,7 @@
     routes_hbm, weights_hbm, tokens_hbm, cotangent_hbm, gate_hbm, up_hbm, down_hbm,
     outs, gg, gu, gd,
     routes, weights, mine, first, second, send,
-    arr, wg, wu, wd, hid, gdy, udy, tt, dd, rl1, rr1, rl2, rr2, yy, zr, ww, uu,
+    arr, wg, wu, wd, hid, gdy, udy, tt, dd, near, last, yy, zr, ww, uu,
     ss, rs, ls,
 ):
     scope = jax.named_scope
@@ -257,7 +257,7 @@
     }
 
     parts = (2, 4)
-    hop_ids = {(g, h, n): fresh() for g in range(2) for h in range(parts[g]) for n in range(4)}
+    hop_ids = {(g, h, n): fresh() for g in range(2) for h in range(parts[g]) for n in range(2)}
 
     def plus(a, b):
         return (a.astype(F32) + b.astype(F32)).astype(BF)
@@ -271,10 +271,10 @@
         rows = rows_h(g, h)
         source = tt.at[g, k, rows, qcols(q, off, half)]
         if n < 2:
-            target = (rl1, rr1)[n].at[g, rows]
+            target = near.at[g, rows, pl.ds(n * half, half)]
         else:
-            target = (rl2 if n % 2 == 0 else rr2).at[g, rows, pl.ds(off, half)]
-        push(out_hop[g, n % 2], hop_ids[g, h, n - 2 if n > 3 else n], source, target, right if n % 2 == 0 else left)
+            target = last.at[g, rows, pl.ds((n % 2) * quart + off, half)]
+        push(out_hop[g, n % 2], hop_ids[g, h, 0 if n < 2 else 1], source, target, right if n % 2 == 0 else left)
 
     def chip_sum(g, n):
         with scope(f"chip_sum_{g}{n}"):
@@ -315,13 +315,12 @@
     def hop_two(g, h):
         with scope(f"hop_two_{g}{h}"):
             rows = rows_h(g, h)
-            got(hop_ids[g, h, 0], rl1.at[g, rows])
+            got(hop_ids[g, h, 0], near.at[g, rows])
             at = qcols(quarters[1], 0, half)
-            tt[g, k, rows, at] = plus(tt[g, k, rows, at], rl1[g, rows])
+            tt[g, k, rows, at] = plus(tt[g, k, rows, at], near[g, rows, :half])
             hop(g, h, 4)
-            got(hop_ids[g, h, 1], rr1.at[g, rows])
             at = qcols(quarters[2], half, half)
-            tt[g, k, rows, at] = plus(tt[g, k, rows, at], rr1[g, rows])
+            tt[g, k, rows, at] = plus(tt[g, k, rows, at], near[g, rows, half:])
             hop(g, h, 5)
 
     def head(zz):
@@ -331,7 +330,7 @@
         return (zz + k) % 2 == 0
 
     home_ids = [fresh() for _ in range(5)]
-    along_ids = {(h, d): fresh() for h in range(parts[1]) for d in range(1, 4)}
+    along_ids = [fresh() for _ in range(parts[1])]
     out_home = [group() for _ in range(5)]
     out_along = {d: group() for d in range(1, 4)}
 
@@ -367,7 +366,7 @@
             def go(wide, d=d, zz=zz):
                 width = 2 * tile if wide else tile
                 push(
-                    out_along[d], along_ids[h, d],
+                    out_along[d], along_ids[h],
                     yy.at[1, rows, pl.ds(pl.multiple_of(head(zz) * tile, 128), width)],
                     zr.at[d - 1, rows, pl.ds(0, width)], dev(y, zh, zz, x, k),
                 )
@@ -377,8 +376,7 @@
     def collect(h):
         def add(wide):
             rows, width = rows_h(1, h), 2 * tile if wide else tile
-            for d in range(1, 4):
-                got(along_ids[h, d], zr.at[d - 1, rows, pl.ds(0, width)])
+            got(along_ids[h], zr.at[:, rows, pl.ds(0, width)])
             for s in range(2 if wide else 1):
                 at = pl.ds(s * tile, tile)
                 total = yy[1, rows, tcols(head(z) + s)].astype(F32)
@@ -396,12 +394,11 @@
     def finish(g, h):
         with scope(f"finish_{g}{h}"):
             rows = rows_h(g, h)
-            got(hop_ids[g, h, 2], rl2.at[g, rows])
-            got(hop_ids[g, h, 3], rr2.at[g, rows])
+            got(hop_ids[g, h, 1], last.at[g, rows])
             yy[g, rows] = (
                 tt[g, k, rows, qcols(x)].astype(F32)
-                + rl2[g, rows].astype(F32)
-                + rr2[g, rows].astype(F32)
+                + last[g, rows, :quart].astype(F32)
+                + last[g, rows, quart:].astype(F32)
             ).astype(BF)
             if g == 1:
                 along(h)
@@ -700,16 +697,14 @@
             pltpu.VMEM((2, grp, hid), BF),
             pltpu.VMEM((2, 2, grp, feat), BF),
             pltpu.VMEM((2, grp, feat), BF),
-            pltpu.VMEM((2, grp, half), BF),
-            pltpu.VMEM((2, grp, half), BF),
             pltpu.VMEM((2, grp, quart), BF),
-            pltpu.VMEM((2, grp, quart), BF),
+            pltpu.VMEM((2, grp, 2 * quart), BF),
             pltpu.VMEM((2, grp, quart), BF),
             pltpu.VMEM((3, grp, 2 * tile), BF),
             pltpu.VMEM((grp, 2 * tile), BF),
             pltpu.VMEM((2, 4, grp, 2 * tile), BF),
             pltpu.SemaphoreType.DMA((29,)),
-            pltpu.SemaphoreType.DMA((97,)),
+            pltpu.SemaphoreType.DMA((77,)),
             pltpu.SemaphoreType.DMA((6,)),
         ],
         compiler_params=pltpu.CompilerParams(

time: 80.6 us -> 80.4 us (level)
  no operation moved by 1% of the time
where the time goes in v6:
time: 80.4 us; the launch traced here: 79.7 us
  Pallas kernels  79 us (98%)
    pallas_call x1, Pallas kernels, on_device(): pl.pallas_call(functools.partial(experts_kernel, dims), out_shape=(pltpu....  76.3 us
    pallas_call x1, Pallas kernels, on_device(): pl.pallas_call(store_kernel, out_shape=(whole, whole, jax.ShapeDtypeStruc...  2.74 us

profile of v6, /device:TPU:1, one launch (start us, length us, event | category | flops | bytes accessed | tf_op | source)
XLA Modules:
  0.0 79.7 jit_solution(6835764584611007735)
XLA Ops:
  0.6 76.3 %experts.1 = (bf16[2,128,3072]{2,1,0:T(8,128)(2,1)S(1)}, bf16[3072,256]{1,0:T(8,128)(2,1)S(1)}, bf16[3072,256]{1,0:T(8,128)(2,1)S(1)}, bf16[256,3072]{1,0:T(8,128)(2,1)S(1)}) custom-call(s32[2,128]{1,0:T(2,128)} %bitcast.11, f32[2,128]{1,0:T(2,128)} %bitcast.12, bf16[128,3072]{1,0:T(8,128)(2,1)} %tokens_hbm.1, bf16[128,3072]{1,0:T(8,128)(2,1)} %cotangent_hbm.1, ...), custom_call_target="tpu_custom_call" | custom-call | tf_op jit(solution)/shard_map/experts/pallas_call | solution.py:674
  76.9 2.7 %store.1 = (bf16[128,3072]{1,0:T(8,128)(2,1)}, bf16[128,3072]{1,0:T(8,128)(2,1)}, bf16[3072,256]{1,0:T(8,128)(2,1)}, bf16[3072,256]{1,0:T(8,128)(2,1)}, bf16[256,3072]{1,0:T(8,128)(2,1)}) custom-call(bf16[2,128,3072]{2,1,0:T(8,128)(2,1)S(1)} %get-tuple-element.14.outs, bf16[3072,256]{1,0:T(8,128)(2,1)S(1)} %get-tuple-element.15.gg, ...), custom_call_target="tpu_custom_call" | custom-call | tf_op jit(solution)/shard_map/store/pallas_call | solution.py:715
